TPU v7x, 32 devices: a whole 2x2x4 slice. The times are simulated.
32 devices in a mesh: span: 8 (over z, y), depth: 4 (over x, core).
Axes of the slice: x: 2, y: 2, z: 4, core: 2. Of those that a mesh axis runs over, the one named last changes fastest.
Arguments:
- part_slab: int32 [4, 65536, 1], P('depth', 'span'), may hold values from 0 to 7; in each aligned block of 8192 rows (0 to 8191, 8192 to 16383, ..., all dimensions but the last counted through in order) at most 2048 rows name the same one
- part_cell: int32 [4, 65536], P('depth', 'span'), may hold values from 0 to 65535
- part_volume: float32 [4, 65536], P('depth', 'span'), may hold values from 0.05 to 0.6
- part_drag: float32 [3, 4, 65536], P(None, 'depth', 'span'), may hold values from -6 to 6
- part_count: int32 [4, 8], P('depth', 'span'), may hold values from 7168 to 8192
- prior_solid: float32 [8, 128, 2048], P(None, 'span', 'depth'), may hold values from 0 to 0.6
- prior_drag: float32 [3, 8, 128, 2048], P(None, None, 'span', 'depth'), may hold values from -4 to 4
Outputs:
- fields: float32 [4, 8, 128, 2048], P(None, None, 'span', 'depth')
- feedback: float32 [4, 4, 65536], P(None, 'depth', 'span')
Inputs may be any that keep to these rules, and one draw needn't show every extreme that they name: `part_slab`: among the 8192 particle slots of one owner device, live or not, no slab is named more than 2048 times; in every draw some device names a slab exactly 2048 times.
All inputs are finite; a program needn't handle non-finite values.
Results may differ from a plain program's by a relative error of at most 0.0003.
Values sent between devices are 32-bit elements; how exact they have to be, the bound alone decides.
A program may use at most 128 MiB of HBM per device.

v0:
```python
import math

import jax
import jax.numpy as jnp
from jax import lax
from jax.sharding import PartitionSpec as P

SWEEPS = 6


NU_WEIGHT = 1.0
PHI_LIMIT = 0.6


def padded_2(array, sides, width):
    for axis, dim in sides:
        count, length = (lax.axis_size(axis), array.shape[dim])
        up = [(i, (i + 1) % count) for i in range(count - 1)]
        down = [(j, i) for i, j in up]
        last = lax.slice_in_dim(array, length - width, length, axis=dim)
        first = lax.slice_in_dim(array, 0, width, axis=dim)
        before = lax.ppermute(last, axis, up)
        after = lax.ppermute(first, axis, down)
        array = jnp.concatenate([before, array, after], axis=dim)
    return array


def relax_once(source, padded):
    beside = padded[:, :, 2:, 1:-1] + padded[:, :, :-2, 1:-1]
    beside = beside + padded[:, :, 1:-1, 2:] + padded[:, :, 1:-1, :-2]
    return (source + NU_WEIGHT * beside) / (1.0 + 4.0 * NU_WEIGHT)


def exact_inner(left, right):
    return lax.dot_general(
        left,
        right,
        (((0,), (0,)), ((), ())),
        precision=lax.Precision.HIGH,
        preferred_element_type=jnp.float32,
    )


def on_device(part_slab, part_cell, part_volume, part_drag, part_count, prior_solid, prior_drag):
    span_size = lax.axis_size("span")
    depth_size = lax.axis_size("depth")
    part_rows = part_cell.shape[1]
    capacity = 2 * part_rows // span_size
    total_slots = span_size * capacity
    layers, width_x, width_y = prior_solid.shape
    cell_total = layers * width_x * width_y
    low_count = math.gcd(cell_total, 128)
    high_count = cell_total // low_count
    part_block = math.gcd(part_rows, 512)
    part_blocks = part_rows // part_block
    slot_block = math.gcd(total_slots, 1024)
    slot_blocks = total_slots // slot_block
    owners = jnp.arange(span_size, dtype=jnp.int32)
    slot_range = jnp.arange(capacity, dtype=jnp.int32)
    high_range = jnp.arange(high_count, dtype=jnp.int32)
    low_range = jnp.arange(low_count, dtype=jnp.int32)
    row_local = jnp.arange(part_block, dtype=jnp.int32)
    lower_tri = (row_local[:, None] > row_local[None, :]).astype(jnp.bfloat16)
    within = jnp.arange(part_rows, dtype=jnp.int32)
    live_flag = within < part_count[0, 0]
    slab_blocks = part_slab[0, :, 0].reshape(part_blocks, part_block)
    live_blocks = live_flag.reshape(part_blocks, part_block)
    payload = jnp.concatenate(
        [part_cell[0].astype(jnp.float32)[None], part_volume, part_drag[:, 0, :]], axis=0
    )
    payload_blocks = payload.reshape(5, part_blocks, part_block).transpose(1, 0, 2)

    def pack_step(carry, inputs):
        offset, packed = carry
        slab_piece, live_piece, load_piece = inputs
        member = (slab_piece[:, None] == owners[None, :]) & live_piece[:, None]
        member_f = member.astype(jnp.float32)
        before = jnp.dot(lower_tri, member.astype(jnp.bfloat16), preferred_element_type=jnp.float32)
        position = jnp.sum((before + offset[None, :]) * member_f, axis=1).astype(jnp.int32)
        slot_hot = (position[:, None] == slot_range[None, :]).astype(jnp.float32)
        pieces = [exact_inner(member_f * load_piece[comp][:, None], slot_hot) for comp in range(5)]
        packed = packed + jnp.stack(pieces, axis=0)
        offset = offset + jnp.sum(member_f, axis=0)
        return ((offset, packed), position)

    start_carry = (
        jnp.zeros((span_size,), jnp.float32),
        jnp.zeros((5, span_size, capacity), jnp.float32),
    )
    (final_offset, packed), positions = lax.scan(
        pack_step, start_carry, (slab_blocks, live_blocks, payload_blocks)
    )
    send_ids = packed[0].astype(jnp.int32).reshape(1, span_size, capacity)
    send_loads = packed[1:]
    recv_ids, recv_loads = (
        lax.all_to_all(send_ids, "span", split_axis=1, concat_axis=1, tiled=True),
        lax.all_to_all(send_loads, "span", split_axis=1, concat_axis=1, tiled=True),
    )
    slot_cells = recv_ids.reshape(slot_blocks, slot_block)
    load_blocks = recv_loads.reshape(4, slot_blocks, slot_block).transpose(1, 0, 2)

    def deposit_step(total, inputs):
        cells, loads = inputs
        high_hot = ((cells // low_count)[:, None] == high_range[None, :]).astype(jnp.float32)
        low_hot = ((cells % low_count)[:, None] == low_range[None, :]).astype(jnp.float32)
        pieces = [exact_inner(high_hot * loads[comp][:, None], low_hot) for comp in range(4)]
        return (total + jnp.stack(pieces, axis=0), 0)

    deposit, unused = lax.scan(
        deposit_step, jnp.zeros((4, high_count, low_count), jnp.float32), (slot_cells, load_blocks)
    )
    deposit = deposit.reshape(4, layers, width_x, width_y)
    target = jnp.concatenate([jnp.minimum(deposit[:1], PHI_LIMIT), deposit[1:]], axis=0)
    smooth = jnp.concatenate([prior_solid[None], prior_drag], axis=0)
    rim_width = 3
    row_ids = (
        lax.axis_index("span") * width_x
        - rim_width
        + jnp.arange(width_x + 2 * rim_width, dtype=jnp.int32)
    )
    col_ids = (
        lax.axis_index("depth") * width_y
        - rim_width
        + jnp.arange(width_y + 2 * rim_width, dtype=jnp.int32)
    )
    row_inside = (row_ids >= 0) & (row_ids < span_size * width_x)
    col_inside = (col_ids >= 0) & (col_ids < depth_size * width_y)
    inside = (row_inside[:, None] & col_inside[None, :]).astype(jnp.float32)
    stacked = padded_2(
        jnp.concatenate([smooth, target], axis=0), (("span", 2), ("depth", 3)), rim_width
    )
    padded = stacked[:4]
    target_wide = stacked[4:]
    for round_index in range(SWEEPS // rim_width):
        if round_index > 0:
            padded = padded_2(smooth, (("span", 2), ("depth", 3)), rim_width)
        for inner_step in range(rim_width):
            edge_offset = inner_step + 1
            size_x = width_x + 2 * (rim_width - edge_offset)
            size_y = width_y + 2 * (rim_width - edge_offset)
            region = target_wide[
                :, :, edge_offset : edge_offset + size_x, edge_offset : edge_offset + size_y
            ]
            keeper = inside[edge_offset : edge_offset + size_x, edge_offset : edge_offset + size_y]
            padded = relax_once(region, padded) * keeper[None, None]
        smooth = padded
    void_fraction = 1.0 - smooth[0]
    fields = jnp.concatenate([void_fraction[None], -smooth[1:] / void_fraction[None]], axis=0)
    field_table = fields.reshape(4, cell_total)
    slot_index = recv_ids.reshape(total_slots).astype(jnp.int32)
    values = field_table[:, slot_index].reshape(4, span_size, capacity)
    returned = lax.all_to_all(values, "span", split_axis=1, concat_axis=1, tiled=True)
    flat_returned = returned.reshape(4, total_slots)
    slab_flat = part_slab[0, :, 0]
    position_flat = jnp.clip(positions.reshape(part_rows), 0, capacity - 1)
    back_index = slab_flat * capacity + position_flat
    picked = flat_returned[:, back_index] * live_flag.astype(jnp.float32)[None, :]
    return (fields, picked.reshape(4, 1, part_rows))


def solution(mesh):
    in_specs = (
        P("depth", "span", None),
        P("depth", "span"),
        P("depth", "span"),
        P(None, "depth", "span"),
        P("depth", "span"),
        P(None, "span", "depth"),
        P(None, None, "span", "depth"),
    )
    out_specs = (P(None, None, "span", "depth"), P(None, "depth", "span"))
    return jax.shard_map(
        on_device, mesh=mesh, in_specs=in_specs, out_specs=out_specs, check_vma=False
    )
```

profile of v0, /device:TPU:1, one launch (start us, length us, event | category | flops | bytes accessed | tf_op | source)
XLA Modules:
  0.0 481.8 jit_solution(172266622983029348)
XLA Ops:
  6.2 107.2 %while.30 = (s32[]{:T(128)}, f32[8]{0:T(128)S(1)}, f32[5,8,2048]{2,1,0:T(8,128)S(1)}, s32[16,512]{1,0:T(8,128)S(1)}, s32[16,512]{1,0:T(8,128)S(1)}, /*index=5*/pred[16,512]{1,0:T(8,128)(4,1)S(1)}, f32[16,5,512]{2,0,1:T(8,128)S(1)}) while((s32[]{:T(128)}, f32[8]{0:T(128)S(1)}, f32[5,8,2048]{2,1,0:T(8,128)S(1)}, ...), condition=%wide.region_3.4_spmd.clone.clone, body=%wide.region_0.3_spmd.clone.sunk.clone | while | flops 261890064 | bytes 1385320 | solution.py:90
  114.1 6.4 %all-to-all-start = ((s32[1,8,2048]{2,0,1:T(1,128)}), s32[1,8,2048]{2,0,1:T(1,128)S(1)}, u32[]{:S(2)}, u32[]{:S(2)}) async-start(s32[1,8,2048]{2,0,1:T(1,128)} %copy.34), calls=%async_computation | async-start | bytes 131072 | tf_op jit(solution)/shard_map/all_to_all | solution.py:96
  122.2 4.0 all-to-all-done
  126.2 3.6 all-to-all-start.1
  130.2 6.6 %all-to-all-done.1 = f32[4,8,2048]{2,0,1:T(4,128)S(1)} async-done(((f32[4,8,2048]{2,0,1:T(4,128)}), f32[4,8,2048]{2,0,1:T(4,128)S(1)}, u32[]{:S(2)}, u32[]{:S(2)}) %all-to-all-start.1) | async-done | bytes 262176 | tf_op jit(solution)/shard_map/all_to_all | solution.py:97
  137.0 113.5 %while.31 = (s32[]{:T(128)}, f32[4,512,128]{2,1,0:T(8,128)S(1)}, s32[16,1024]{1,0:T(8,128)S(1)}, f32[16,4,1024]{2,0,1:T(8,128)S(1)}) while((s32[]{:T(128)}, f32[4,512,128]{2,1,0:T(8,128)S(1)}, s32[16,1024]{1,0:T(8,128)S(1)}, f32[16,4,1024]{2,0,1:T(8,128)S(1)}) %tuple.99), condition=%wide.region_5.6_spmd.clone.clone, body=%wide.region_4.5_spmd.clone.sunk.clone | while | flops 1616661504 | bytes 4296823 | solution.py:109
  137.1 1.7 fusion.203
  145.9 1.7 fusion.204
  147.6 1.7 fusion.205
  151.3 1.7 fusion.203
  153.0 1.7 fusion.204
  154.7 1.7 fusion.205
  156.4 1.7 fusion.202
  160.1 1.7 fusion.204
  161.8 1.7 fusion.205
  170.6 1.7 fusion.202
  179.7 1.7 fusion.203
  181.4 1.7 fusion.204
  183.1 1.7 fusion.205
  252.1 1.9 collective-permute-start
  257.0 10.4 %collective-permute-done = f32[8,8,3,512]{3,1,2,0:T(8,128)S(1)} collective-permute-done((f32[8,8,3,512]{3,1,2,0:T(8,128)S(1)}, f32[8,8,3,512]{3,1,2,0:T(8,128)S(1)}, u32[]{:S(2)}, u32[]{:S(2)}) %collective-permute-start) | collective-permute-done | bytes 393248 | tf_op jit(solution)/shard_map/ppermute | solution.py:22
  269.5 2.3 copy.42
  271.8 7.5 %collective-permute-start.2 = (f32[8,8,22,3]{2,1,3,0:T(8,128)}, f32[8,8,22,3]{2,1,3,0:T(8,128)}, u32[]{:S(2)}, u32[]{:S(2)}) collective-permute-start(f32[8,8,22,3]{2,1,3,0:T(8,128)} %copy.42), channel_id=1, source_target_pairs={{0,1},{1,2},{2,3},{4,5},{5,6},{6,7},{8,9},{9,10},{10,11},{12,13},{... | collective-permute-start | bytes 50696 | tf_op jit(solution)/shard_map/ppermute | solution.py:22
  279.3 2.2 copy.43
  281.5 2.1 collective-permute-start.3
  283.7 2.3 copy.44
  286.0 1.8 collective-permute-done.3
  287.8 2.3 copy.45
  290.0 5.1 %pad_maximum_fusion = f32[8,8,22,518]{3,2,1,0:T(8,128)S(1)} fusion(f32[8,8,22,3]{3,2,1,0:T(8,128)} %copy.45, f32[8,8,3,512]{3,2,1,0:T(4,128)} %copy-done.1, f32[3,8,16,512]{3,2,1,0:T(8,128)S(1)} %slice.204, f32[1,8,16,512]{3,2,1,0:T(8,128)S(1)} %min.29, f32[3,8,16,512]{3,2,1,0:T(8,128)S(1)} %copy-done, f32[1,8,16,512]{3,2,1,0:T(8,128)} %bitcast.178, ...), kind=kLoop, calls=%fused_computation.127 | loop fusion | flops 5105408 | bytes 5834752 | tf_op jit(solution)/shard_map/concatenate | solution.py:24
  295.1 2.5 fusion.127
  297.7 2.5 fusion.125
  301.3 4.1 collective-permute-start.4
  306.8 8.1 %collective-permute-done.4 = f32[4,8,3,512]{3,2,1,0:T(4,128)S(1)} collective-permute-done((f32[4,8,3,512]{3,2,1,0:T(4,128)S(1)}, f32[4,8,3,512]{3,2,1,0:T(4,128)S(1)}, u32[]{:S(2)}, u32[]{:S(2)}) %collective-permute-start.4) | collective-permute-done | bytes 196640 | tf_op jit(solution)/shard_map/ppermute | solution.py:22
  315.2 3.4 collective-permute-start.6
  318.6 2.2 collective-permute-start.7
  320.8 2.5 collective-permute-done.6
  323.3 4.4 collective-permute-done.7
  328.9 2.5 fusion.123
  331.4 2.5 fusion.121
  336.4 16.0 %copy.46 = f32[4,65536]{0,1:T(8,128)} copy(f32[4,65536]{1,0:T(4,128)S(1)} %pad_maximum_fusion.3) | data formatting | bytes 2097152 | tf_op jit(solution)/shard_map/concatenate | solution.py:148
  352.4 65.3 %gather_fusion = f32[16384,4]{1,0:T(8,128)} fusion(f32[4,65536]{0,1:T(8,128)} %copy.46, s32[16384]{0:T(1024)S(1)} %broadcast_clamp_fusion), kind=kCustom, calls=%fused_computation | custom fusion | bytes 589824 | tf_op jit(solution)/shard_map/gather | solution.py:151
  417.7 5.9 %copy.47 = f32[4,8,2048]{2,0,1:T(4,128)} copy(f32[4,8,2048]{0,2,1:T(8,128)} %bitcast.175) | data formatting | bytes 524288 | tf_op jit(solution)/shard_map/reshape | solution.py:151
  423.6 7.2 %all-to-all-start.2 = ((f32[4,8,2048]{2,0,1:T(4,128)}), f32[4,8,2048]{2,0,1:T(4,128)S(1)}, u32[]{:S(2)}, u32[]{:S(2)}) async-start(f32[4,8,2048]{2,0,1:T(4,128)} %copy.47), calls=%async_computation.2 | async-start | bytes 524288 | tf_op jit(solution)/shard_map/all_to_all | solution.py:152
  431.9 6.0 %all-to-all-done.2 = f32[4,8,2048]{2,0,1:T(4,128)S(1)} async-done(((f32[4,8,2048]{2,0,1:T(4,128)}), f32[4,8,2048]{2,0,1:T(4,128)S(1)}, u32[]{:S(2)}, u32[]{:S(2)}) %all-to-all-start.2) | async-done | bytes 262176 | tf_op jit(solution)/shard_map/all_to_all | solution.py:152
  437.8 4.6 copy.48
  442.5 31.2 %gather_fusion.1 = f32[8192,4]{1,0:T(8,128)} fusion(f32[4,16384]{0,1:T(8,128)} %bitcast.174, s32[8192]{0:T(1024)S(1)} %broadcast_clamp_fusion.1), kind=kCustom, calls=%fused_computation.1 | custom fusion | bytes 294912 | tf_op jit(solution)/shard_map/gather | solution.py:157
  473.7 4.2 bitcast_multiply_fusion
  477.8 3.5 copy.49
  (418 shorter events, 218.5 us)
Async XLA Ops:
  6.2 114.4 %copy-start.6 = (s32[1,8192,1]{1,2,0:T(1,128)S(1)}, s32[1,8192,1]{1,2,0:T(1,128)}, u32[]{:S(2)}) copy-start(s32[1,8192,1]{1,2,0:T(1,128)} %param.11) | copy-start | bytes 98308
  114.1 12.1 %all-to-all-start = ((s32[1,8,2048]{2,0,1:T(1,128)}), s32[1,8,2048]{2,0,1:T(1,128)S(1)}, u32[]{:S(2)}, u32[]{:S(2)}) async-start(s32[1,8,2048]{2,0,1:T(1,128)} %copy.34), calls=%async_computation | async-start | bytes 131072 | tf_op jit(solution)/shard_map/all_to_all | solution.py:96
  126.2 10.6 %all-to-all-start.1 = ((f32[4,8,2048]{2,0,1:T(4,128)}), f32[4,8,2048]{2,0,1:T(4,128)S(1)}, u32[]{:S(2)}, u32[]{:S(2)}) async-start(f32[4,8,2048]{2,0,1:T(4,128)} %slice.257), calls=%async_computation.1 | async-start | bytes 524288 | tf_op jit(solution)/shard_map/all_to_all | solution.py:97
  250.6 1.1 copy-start
  250.6 1.2 copy-start.2
  252.0 15.9 %copy-start.3 = (f32[8,16,512]{2,1,0:T(8,128)S(1)}, f32[8,16,512]{2,1,0:T(8,128)}, u32[]{:S(2)}) copy-start(f32[8,16,512]{2,1,0:T(8,128)} %param.16) | copy-start | bytes 786436
  252.1 15.2 %collective-permute-start = (f32[8,8,3,512]{3,1,2,0:T(8,128)S(1)}, f32[8,8,3,512]{3,1,2,0:T(8,128)S(1)}, u32[]{:S(2)}, u32[]{:S(2)}) collective-permute-start(f32[8,8,3,512]{3,1,2,0:T(8,128)S(1)} %copy.38), channel_id=1, source_target_pairs={{0,4},{4,8},{8,12},{12,16},{16,20},{20,24},{24,28},{1,5},{5,9},{9,... | collective-permute-start | bytes 1179656 | tf_op jit(solution)/shard_map/ppermute | solution.py:22
  254.2 13.4 %collective-permute-start.1 = (f32[8,8,3,512]{3,1,2,0:T(8,128)S(1)}, f32[8,8,3,512]{3,1,2,0:T(8,128)S(1)}, u32[]{:S(2)}, u32[]{:S(2)}) collective-permute-start(f32[8,8,3,512]{3,1,2,0:T(8,128)S(1)} %copy.39), channel_id=1, source_target_pairs={{4,0},{8,4},{12,8},{16,12},{20,16},{24,20},{28,24},{5,1},{9,5},{13... | collective-permute-start | bytes 1179656 | tf_op jit(solution)/shard_map/ppermute | solution.py:23
  267.9 1.6 copy-start.1
  271.8 11.9 %collective-permute-start.2 = (f32[8,8,22,3]{2,1,3,0:T(8,128)}, f32[8,8,22,3]{2,1,3,0:T(8,128)}, u32[]{:S(2)}, u32[]{:S(2)}) collective-permute-start(f32[8,8,22,3]{2,1,3,0:T(8,128)} %copy.42), channel_id=1, source_target_pairs={{0,1},{1,2},{2,3},{4,5},{5,6},{6,7},{8,9},{9,10},{10,11},{12,13},{... | collective-permute-start | bytes 50696 | tf_op jit(solution)/shard_map/ppermute | solution.py:22
  281.5 6.2 %collective-permute-start.3 = (f32[8,8,22,3]{2,1,3,0:T(8,128)}, f32[8,8,22,3]{2,1,3,0:T(8,128)}, u32[]{:S(2)}, u32[]{:S(2)}) collective-permute-start(f32[8,8,22,3]{2,1,3,0:T(8,128)} %copy.43), channel_id=1, source_target_pairs={{1,0},{2,1},{3,2},{5,4},{6,5},{7,6},{9,8},{10,9},{11,10},{13,12},{... | collective-permute-start | bytes 50696 | tf_op jit(solution)/shard_map/ppermute | solution.py:23
  295.1 2.5 copy-start.4
  297.6 2.5 copy-start.5
  301.3 13.6 %collective-permute-start.4 = (f32[4,8,3,512]{3,2,1,0:T(4,128)S(1)}, f32[4,8,3,512]{3,2,1,0:T(4,128)S(1)}, u32[]{:S(2)}, u32[]{:S(2)}) collective-permute-start(f32[4,8,3,512]{3,2,1,0:T(4,128)S(1)} %get-tuple-element.271), channel_id=1, source_target_pairs={{0,4},{4,8},{8,12},{12,16},{16,20},{20,24},{24,28},{1,5},{5,9},{9,... | collective-permute-start | bytes 589832 | tf_op jit(solution)/shard_map/ppermute | solution.py:22
  305.4 9.5 %collective-permute-start.5 = (f32[4,8,3,512]{3,2,1,0:T(4,128)S(1)}, f32[4,8,3,512]{3,2,1,0:T(4,128)S(1)}, u32[]{:S(2)}, u32[]{:S(2)}) collective-permute-start(f32[4,8,3,512]{3,2,1,0:T(4,128)S(1)} %get-tuple-element.272), channel_id=1, source_target_pairs={{4,0},{8,4},{12,8},{16,12},{20,16},{24,20},{28,24},{5,1},{9,5},{13... | collective-permute-start | bytes 589832 | tf_op jit(solution)/shard_map/ppermute | solution.py:23
  315.2 8.1 %collective-permute-start.6 = (f32[4,8,22,3]{3,2,1,0:T(8,128)S(1)}, f32[4,8,22,3]{3,2,1,0:T(8,128)S(1)}, u32[]{:S(2)}, u32[]{:S(2)}) collective-permute-start(f32[4,8,22,3]{3,2,1,0:T(8,128)S(1)} %get-tuple-element.267), channel_id=1, source_target_pairs={{0,1},{1,2},{2,3},{4,5},{5,6},{6,7},{8,9},{9,10},{10,11},{12,13},{... | collective-permute-start | bytes 25352 | tf_op jit(solution)/shard_map/ppermute | solution.py:22
  318.6 9.1 %collective-permute-start.7 = (f32[4,8,22,3]{3,2,1,0:T(8,128)S(1)}, f32[4,8,22,3]{3,2,1,0:T(8,128)S(1)}, u32[]{:S(2)}, u32[]{:S(2)}) collective-permute-start(f32[4,8,22,3]{3,2,1,0:T(8,128)S(1)} %get-tuple-element.268), channel_id=1, source_target_pairs={{1,0},{2,1},{3,2},{5,4},{6,5},{7,6},{9,8},{10,9},{11,10},{13,12},{... | collective-permute-start | bytes 25352 | tf_op jit(solution)/shard_map/ppermute | solution.py:23
  417.7 13.1 %copy-start.7 = (s32[8192,1]{0,1:T(1,128)S(1)}, s32[8192,1]{0,1:T(1,128)}, u32[]{:S(2)}) copy-start(s32[8192,1]{0,1:T(1,128)} %compare_select_fusion.1) | copy-start | bytes 98308
  423.6 14.3 %all-to-all-start.2 = ((f32[4,8,2048]{2,0,1:T(4,128)}), f32[4,8,2048]{2,0,1:T(4,128)S(1)}, u32[]{:S(2)}, u32[]{:S(2)}) async-start(f32[4,8,2048]{2,0,1:T(4,128)} %copy.47), calls=%async_computation.2 | async-start | bytes 524288 | tf_op jit(solution)/shard_map/all_to_all | solution.py:152
where the time goes:
time: 488 us; the launch traced here: 482 us
  matrix products  208 us (43%)
  local copies, waits for them, and re-layouts  144 us (30%)
  waiting for transfers between devices  43.8 us (9%)
  starting transfers between devices  41 us (8%)
  other arithmetic  40.2 us (8%)
    dot_general x144, matrix products, exact_inner(): lax.dot_general(left, right, (((0,), (0,)), ((), ())), precision=lax.Prec...  204 us
    gather x1, local copies, waits for them, and re-layouts, on_device(): values = field_table[:, slot_index].reshape(4, span_size, capacity)  65.3 us
    gather x1, local copies, waits for them, and re-layouts, on_device(): flat_returned[:, back_index] * live_flag.astype(jnp.float32)[None, :]  31.2 us
    ppermute x4, waiting for transfers between devices, padded_2(): before = lax.ppermute(last, axis, up)  21 us
    ppermute x4, starting transfers between devices, padded_2(): before = lax.ppermute(last, axis, up)  16.9 us
    concatenate x1, local copies, waits for them, and re-layouts, on_device(): jnp.concatenate([void_fraction[None], -smooth[1:] / void_fraction[None]],...  16 us
    mul x9, other arithmetic, on_device(): padded = relax_once(region, padded) * keeper[None, None]  13.6 us
  transfers between devices with their start and end apart: 11, of which 8 were waited for; matrix products, arithmetic and copies ran while one was open for 2% of the time, Pallas kernels for 0%

commit v1 on v0

v1 whole, which is shorter than its diff:
```python
import functools
import math

import jax
import jax.numpy as jnp
from jax import lax
from jax.experimental import pallas as pl
from jax.experimental.pallas import tpu as pltpu
from jax.sharding import PartitionSpec as P

SWEEPS = 6
NU_WEIGHT = 1.0
PHI_LIMIT = 0.6
BF = jnp.bfloat16
F32 = jnp.float32


def two_parts(value):
    high = value.astype(BF)
    return high, (value - high.astype(F32)).astype(BF)


def hot_of(index, count):
    rows = lax.broadcasted_iota(jnp.int32, (count, index.shape[1]), 0)
    return jnp.where(rows == index, 1.0, 0.0).astype(BF)


def nt_dot(left, right):
    return lax.dot_general(left, right, (((1,), (1,)), ((), ())), preferred_element_type=F32)


def spread(values, row, col, rows, cols):
    mask = lax.broadcasted_iota(jnp.int32, (rows, row.shape[1]), 0) == row
    hot = hot_of(col, cols)
    total = None
    for part in range(2):
        left = jnp.concatenate(
            [jnp.where(mask, two_parts(v)[part].astype(F32), 0.0).astype(BF) for v in values], axis=0
        )
        term = nt_dot(left, hot)
        total = term if total is None else total + term
    return total


def pick(high, low, row, col, rows, cols):
    hot = hot_of(col, cols)
    wide = jnp.dot(high, hot, preferred_element_type=F32)
    wide = wide + jnp.dot(low, hot, preferred_element_type=F32)
    mask = lax.broadcasted_iota(jnp.int32, (rows, row.shape[1]), 0) == row
    comps = high.shape[0] // rows
    found = [
        jnp.sum(jnp.where(mask, wide[c * rows : (c + 1) * rows], 0.0), axis=0, keepdims=True)
        for c in range(comps)
    ]
    return found


def pack_kernel(span, cap, block, count, slab, cell, volume, drag, out, slots):
    rows, cols = out.shape[1:]
    part_rows = slab.shape[1]
    out[...] = jnp.zeros_like(out)
    before_lane = lax.broadcasted_iota(jnp.int32, (block, block), 0)
    this_lane = lax.broadcasted_iota(jnp.int32, (block, block), 1)
    tri = jnp.where(before_lane < this_lane, 1.0, 0.0).astype(BF)
    live_count = count[0, 0]

    def step(b, offset):
        lanes = pl.ds(pl.multiple_of(b * block, block), block)
        sl = slab[:, lanes]
        live = b * block + lax.broadcasted_iota(jnp.int32, (1, block), 1) < live_count
        key = jnp.where(live, sl, -1)
        member = jnp.where(lax.broadcasted_iota(jnp.int32, (span, block), 0) == key, 1.0, 0.0)
        before = jnp.dot(member.astype(BF), tri, preferred_element_type=F32)
        place = jnp.sum(member * (before + offset), axis=0, keepdims=True).astype(jnp.int32)
        slot = jnp.where(live, sl * cap + place, -1)
        slots[:, lanes] = slot
        row = lax.shift_right_arithmetic(slot, int(math.log2(cols)))
        col = lax.bitwise_and(slot, cols - 1)
        values = [cell[:, lanes].astype(F32), volume[:, lanes]]
        values += [drag[c, :, lanes] for c in range(drag.shape[0])]
        out[...] += spread(values, row, col, rows, cols).reshape(out.shape)
        return offset + jnp.sum(member, axis=1, keepdims=True)

    lax.fori_loop(0, part_rows // block, step, jnp.zeros((span, 1), F32))


def deposit_kernel(group, recv, out):
    comps, rows, cols = out.shape
    out[...] = jnp.zeros_like(out)

    def step(g, carry):
        lines = pl.ds(pl.multiple_of(g * group, group), group)
        block = [recv[c, lines, :] for c in range(comps + 1)]
        flat = [
            jnp.concatenate([b[j : j + 1] for j in range(group)], axis=1) for b in block
        ]
        ids = flat[0].astype(jnp.int32)
        row = lax.shift_right_arithmetic(ids, int(math.log2(cols)))
        col = lax.bitwise_and(ids, cols - 1)
        out[...] += spread(flat[1:], row, col, rows, cols).reshape(out.shape)
        return carry

    lax.fori_loop(0, recv.shape[1] // group, step, 0)
    out[0] = jnp.minimum(out[0], PHI_LIMIT)


def gather_kernel(group, fields, ids_ref, out, high, low):
    comps, rows, cols = fields.shape
    table = fields[...].reshape(comps * rows, cols)
    high[...], low[...] = two_parts(table)

    def step(g, carry):
        lines = pl.ds(pl.multiple_of(g * group, group), group)
        block = ids_ref[0, lines, :].astype(jnp.int32)
        found = []
        for j in range(group):
            ids = block[j : j + 1]
            row = lax.shift_right_arithmetic(ids, int(math.log2(cols)))
            col = lax.bitwise_and(ids, cols - 1)
            found.append(pick(high[...], low[...], row, col, rows, cols))
        for c in range(comps):
            out[c, lines, :] = jnp.concatenate([f[c] for f in found], axis=0)
        return carry

    lax.fori_loop(0, ids_ref.shape[1] // group, step, 0)


def unpack_kernel(block, table_ref, slots, out):
    comps, rows, cols = table_ref.shape
    high, low = two_parts(table_ref[...].reshape(comps * rows, cols))

    def step(b, carry):
        lanes = pl.ds(pl.multiple_of(b * block, block), block)
        slot = slots[:, lanes]
        row = lax.shift_right_arithmetic(slot, int(math.log2(cols)))
        col = lax.bitwise_and(slot, cols - 1)
        found = pick(high, low, row, col, rows, cols)
        for c in range(comps):
            out[c, :, lanes] = found[c]
        return carry

    lax.fori_loop(0, slots.shape[1] // block, step, 0)


def padded_2(array, sides, width):
    for axis, dim in sides:
        count, length = (lax.axis_size(axis), array.shape[dim])
        up = [(i, (i + 1) % count) for i in range(count - 1)]
        down = [(j, i) for i, j in up]
        last = lax.slice_in_dim(array, length - width, length, axis=dim)
        first = lax.slice_in_dim(array, 0, width, axis=dim)
        before = lax.ppermute(last, axis, up)
        after = lax.ppermute(first, axis, down)
        array = jnp.concatenate([before, array, after], axis=dim)
    return array


def relax_once(source, padded):
    beside = padded[:, :, 2:, 1:-1] + padded[:, :, :-2, 1:-1]
    beside = beside + padded[:, :, 1:-1, 2:] + padded[:, :, 1:-1, :-2]
    return (source + NU_WEIGHT * beside) / (1.0 + 4.0 * NU_WEIGHT)


VMEM = pl.BlockSpec(memory_space=pltpu.VMEM)
SMEM = pl.BlockSpec(memory_space=pltpu.SMEM)
LIMIT = pltpu.CompilerParams(vmem_limit_bytes=48 * 1024 * 1024)


def on_device(part_slab, part_cell, part_volume, part_drag, part_count, prior_solid, prior_drag):
    span_size = lax.axis_size("span")
    depth_size = lax.axis_size("depth")
    part_rows = part_cell.shape[1]
    cap = 2 * part_rows // span_size
    layers, width_x, width_y = prior_solid.shape
    cols = min(256, cap)
    lines = span_size * cap // cols
    block = math.gcd(part_rows, 512)
    packed, slots = pl.pallas_call(
        functools.partial(pack_kernel, span_size, cap, block),
        out_shape=(
            jax.ShapeDtypeStruct((5, lines, cols), F32),
            jax.ShapeDtypeStruct((1, part_rows), jnp.int32),
        ),
        in_specs=[SMEM] + [VMEM] * 4,
        out_specs=(VMEM, VMEM),
        compiler_params=LIMIT,
        name="pack",
    )(part_count, part_slab.reshape(1, part_rows), part_cell, part_volume, part_drag)
    per = lines // span_size
    recv = lax.all_to_all(
        packed.reshape(5, span_size, per, cols), "span", split_axis=1, concat_axis=1, tiled=True
    ).reshape(5, lines, cols)
    grid_rows = layers * width_x
    target = pl.pallas_call(
        functools.partial(deposit_kernel, 8),
        out_shape=jax.ShapeDtypeStruct((4, grid_rows, width_y), F32),
        in_specs=[VMEM],
        out_specs=VMEM,
        compiler_params=LIMIT,
        name="deposit",
    )(recv)
    target = target.reshape(4, layers, width_x, width_y)
    smooth = jnp.concatenate([prior_solid[None], prior_drag], axis=0)
    rim_width = 3
    row_ids = (
        lax.axis_index("span") * width_x
        - rim_width
        + jnp.arange(width_x + 2 * rim_width, dtype=jnp.int32)
    )
    col_ids = (
        lax.axis_index("depth") * width_y
        - rim_width
        + jnp.arange(width_y + 2 * rim_width, dtype=jnp.int32)
    )
    row_inside = (row_ids >= 0) & (row_ids < span_size * width_x)
    col_inside = (col_ids >= 0) & (col_ids < depth_size * width_y)
    inside = (row_inside[:, None] & col_inside[None, :]).astype(jnp.float32)
    stacked = padded_2(
        jnp.concatenate([smooth, target], axis=0), (("span", 2), ("depth", 3)), rim_width
    )
    padded = stacked[:4]
    target_wide = stacked[4:]
    for round_index in range(SWEEPS // rim_width):
        if round_index > 0:
            padded = padded_2(smooth, (("span", 2), ("depth", 3)), rim_width)
        for inner_step in range(rim_width):
            edge_offset = inner_step + 1
            size_x = width_x + 2 * (rim_width - edge_offset)
            size_y = width_y + 2 * (rim_width - edge_offset)
            region = target_wide[
                :, :, edge_offset : edge_offset + size_x, edge_offset : edge_offset + size_y
            ]
            keeper = inside[edge_offset : edge_offset + size_x, edge_offset : edge_offset + size_y]
            padded = relax_once(region, padded) * keeper[None, None]
        smooth = padded
    void_fraction = 1.0 - smooth[0]
    fields = jnp.concatenate([void_fraction[None], -smooth[1:] / void_fraction[None]], axis=0)
    table = fields.reshape(4, grid_rows, width_y)
    values = pl.pallas_call(
        functools.partial(gather_kernel, 8),
        out_shape=jax.ShapeDtypeStruct((4, lines, cols), F32),
        in_specs=[VMEM] * 2,
        out_specs=VMEM,
        scratch_shapes=[pltpu.VMEM((4 * grid_rows, width_y), BF)] * 2,
        compiler_params=LIMIT,
        name="gather",
    )(table, recv)
    returned = lax.all_to_all(
        values.reshape(4, span_size, per, cols), "span", split_axis=1, concat_axis=1, tiled=True
    ).reshape(4, lines, cols)
    feedback = pl.pallas_call(
        functools.partial(unpack_kernel, block),
        out_shape=jax.ShapeDtypeStruct((4, 1, part_rows), F32),
        in_specs=[VMEM] * 2,
        out_specs=VMEM,
        compiler_params=LIMIT,
        name="unpack",
    )(returned, slots)
    return (fields, feedback)


def solution(mesh):
    in_specs = (
        P("depth", "span", None),
        P("depth", "span"),
        P("depth", "span"),
        P(None, "depth", "span"),
        P("depth", "span"),
        P(None, "span", "depth"),
        P(None, None, "span", "depth"),
    )
    out_specs = (P(None, None, "span", "depth"), P(None, "depth", "span"))
    return jax.shard_map(
        on_device, mesh=mesh, in_specs=in_specs, out_specs=out_specs, check_vma=False
    )
```

time: 488 us -> 213 us (0.44); the launches traced: 482 us -> 212 us
  matrix products: 208 us -> 0 us
  local copies, waits for them, and re-layouts: 144 us -> 53.7 us
  Pallas kernels: 0 us -> 58 us
  waiting for transfers between devices: 43.8 us -> 27.3 us
  other arithmetic: 40.2 us -> 35.1 us
    dot_general x160 -> x0, matrix products: 208 us -> none  [the longest x144 204 us: exact_inner(): lax.dot_general(left, right, (((0,), (0,)), ((), ())), precision=lax.Prec...]
    gather x2 -> x0, local copies, waits for them, and re-layouts: 96.5 us -> none  [the longest x1 65.3 us: on_device(): values = field_table[:, slot_index].reshape(4, span_size, capacity)]
    pallas_call x0 -> x4, Pallas kernels: none -> 58 us  [the longest x1 22 us: on_device(): pl.pallas_call(functools.partial(gather_kernel, 8), out_shape=jax.ShapeDt...]
    concatenate x2 -> x3, other arithmetic: 6.27 us -> 21.5 us  [padded_2(): array = jnp.concatenate([before, array, after], axis=dim)]
    ppermute x4, waiting for transfers between devices: 21 us -> 9.37 us  [padded_2(): before = lax.ppermute(last, axis, up)]
    concatenate x1, local copies, waits for them, and re-layouts: 0.07 us -> 8.61 us  [on_device(): jnp.concatenate([smooth, target], axis=0)]
    ppermute x2, local copies, waits for them, and re-layouts: 2.54 us -> 10.2 us  [padded_2(): before = lax.ppermute(last, axis, up)]
    ppermute x2, local copies, waits for them, and re-layouts: 2.53 us -> 10.1 us  [padded_2(): after = lax.ppermute(first, axis, down)]
  transfers between devices with their start and end apart: 11 -> 10, of which waited for: 8 -> 6; matrix products, arithmetic and copies ran while one was open for 2% -> 16% of each run, Pallas kernels for 0% -> 0%
where the time goes in v1:
time: 213 us; the launch traced here: 212 us
  Pallas kernels  58 us (27%)
  local copies, waits for them, and re-layouts  53.7 us (25%)
  starting transfers between devices  36.3 us (17%)
  other arithmetic  35.1 us (16%)
  waiting for transfers between devices  27.3 us (13%)
    pallas_call x1, Pallas kernels, on_device(): pl.pallas_call(functools.partial(gather_kernel, 8), out_shape=jax.ShapeDt...  22 us
    concatenate x3, other arithmetic, padded_2(): array = jnp.concatenate([before, array, after], axis=dim)  21.5 us
    pallas_call x1, Pallas kernels, on_device(): pl.pallas_call(functools.partial(deposit_kernel, 8), out_shape=jax.ShapeD...  20.1 us
    ppermute x4, starting transfers between devices, padded_2(): before = lax.ppermute(last, axis, up)  19.7 us
    concatenate x1, local copies, waits for them, and re-layouts, padded_2(): array = jnp.concatenate([before, array, after], axis=dim)  11.6 us
    unnamed x20, local copies, waits for them, and re-layouts  10.7 us
    ppermute x2, local copies, waits for them, and re-layouts, padded_2(): before = lax.ppermute(last, axis, up)  10.2 us
    ppermute x2, local copies, waits for them, and re-layouts, padded_2(): after = lax.ppermute(first, axis, down)  10.1 us
  transfers between devices with their start and end apart: 10, of which 6 were waited for; matrix products, arithmetic and copies ran while one was open for 16% of the time, Pallas kernels for 0%

profile of v1, /device:TPU:1, one launch (start us, length us, event | category | flops | bytes accessed | tf_op | source)
XLA Modules:
  0.0 212.1 jit_solution(9698086066571068543)
XLA Ops:
  1.3 0.9 copy-done
  2.2 0.8 copy-done.1
  2.9 0.8 copy-done.2
  3.7 0.8 copy-done.3
  4.4 9.8 %pack.1 = (f32[5,64,256]{2,1,0:T(8,128)S(1)}, s32[1,8192]{1,0:T(1,128)S(1)}) custom-call(s32[1,1]{1,0:T(1,128)S(6)} %copy.64.count, s32[1,8192]{1,0:T(1,128)S(1)} %bitcast.23, s32[1,8192]{1,0:T(1,128)S(1)} %copy-done.2, f32[1,8192]{1,0:T(1,128)S(1)} %copy-done.3, f32[3,1,8192]{2,1,0:T(1,128)S(1)} %copy-done), custom_call_target="tpu_custom_call" | custom-call | tf_op jit(solution)/shard_map/pack/pallas_call | solution.py:178
  14.3 0.7 copy.38
  15.0 6.4 %all-to-all-start = ((f32[5,8,8,256]{3,2,0,1:T(8,128)}), f32[5,8,8,256]{3,2,0,1:T(8,128)S(1)}, u32[]{:S(2)}, u32[]{:S(2)}) async-start(f32[5,8,8,256]{3,2,0,1:T(8,128)} %copy.38), calls=%async_computation | async-start | bytes 655360 | tf_op jit(solution)/shard_map/all_to_all | solution.py:190
  21.4 0.7 and_convert_fusion
  22.1 7.6 %all-to-all-done = f32[5,8,8,256]{3,2,0,1:T(8,128)S(1)} async-done(((f32[5,8,8,256]{3,2,0,1:T(8,128)}), f32[5,8,8,256]{3,2,0,1:T(8,128)S(1)}, u32[]{:S(2)}, u32[]{:S(2)}) %all-to-all-start) | async-done | bytes 327712 | tf_op jit(solution)/shard_map/all_to_all | solution.py:190
  29.7 20.1 %deposit.1 = f32[4,128,512]{2,1,0:T(8,128)S(1)} custom-call(f32[5,64,256]{2,1,0:T(8,128)S(1)} %bitcast.18), custom_call_target="tpu_custom_call" | custom-call | tf_op jit(solution)/shard_map/deposit/pallas_call | solution.py:194
  49.8 1.4 pad_maximum_fusion.2
  51.5 0.9 copy.56
  52.4 4.2 %collective-permute-start = (f32[8,8,3,512]{3,1,2,0:T(8,128)}, f32[8,8,3,512]{3,1,2,0:T(8,128)}, u32[]{:S(2)}, u32[]{:S(2)}) collective-permute-start(f32[8,8,3,512]{3,1,2,0:T(8,128)} %copy.56), channel_id=1, source_target_pairs={{0,4},{4,8},{8,12},{12,16},{16,20},{20,24},{24,28},{1,5},{5,9},{9,... | collective-permute-start | bytes 1179656 | tf_op jit(solution)/shard_map/ppermute | solution.py:152
  56.6 0.9 copy.57
  57.5 1.3 collective-permute-start.1
  58.8 0.7 slice_multiply_fusion.1
  59.5 0.7 slice_multiply_fusion
  60.2 8.6 %copy.43 = f32[8,8,16,512]{2,1,3,0:T(8,128)} copy(f32[8,8,16,512]{3,2,1,0:T(8,128)S(1)} %pad_maximum_fusion.2) | data formatting | bytes 4194304 | tf_op jit(solution)/shard_map/concatenate | solution.py:219
  68.8 1.7 collective-permute-done
  70.5 9.7 %copy.42 = f32[8,8,3,512]{2,1,3,0:T(8,128)} copy(f32[8,8,3,512]{3,1,2,0:T(8,128)} %collective-permute-done) | data formatting | bytes 786432 | tf_op jit(solution)/shard_map/ppermute | solution.py:152
  80.2 9.6 %copy.44 = f32[8,8,3,512]{2,1,3,0:T(8,128)} copy(f32[8,8,3,512]{3,1,2,0:T(8,128)} %collective-permute-done.1) | data formatting | bytes 786432 | tf_op jit(solution)/shard_map/ppermute | solution.py:153
  89.8 17.9 %pad_maximum_fusion = f32[8,8,22,512]{2,1,3,0:T(8,128)S(1)} fusion(f32[8,8,3,512]{2,1,3,0:T(8,128)} %copy.44, f32[8,8,16,512]{2,1,3,0:T(8,128)} %copy.43, f32[8,8,3,512]{2,1,3,0:T(8,128)} %copy.42), kind=kLoop, calls=%fused_computation | loop fusion | flops 1441792 | bytes 5767168 | tf_op jit(solution)/shard_map/concatenate | solution.py:154
  107.7 5.7 %copy-done.4 = f32[8,8,22,512]{2,1,3,0:T(8,128)} copy-done((f32[8,8,22,512]{2,1,3,0:T(8,128)}, f32[8,8,22,512]{2,1,3,0:T(8,128)S(1)}, u32[]{:S(2)}) %copy-start.4) | copy-done | bytes 2883608
  113.4 6.7 %collective-permute-start.2 = (f32[8,8,22,3]{2,1,3,0:T(8,128)S(1)}, f32[8,8,22,3]{2,1,3,0:T(8,128)S(1)}, u32[]{:S(2)}, u32[]{:S(2)}) collective-permute-start(f32[8,8,22,3]{2,1,3,0:T(8,128)S(1)} %get-tuple-element.8), channel_id=1, source_target_pairs={{0,1},{1,2},{2,3},{4,5},{5,6},{6,7},{8,9},{9,10},{10,11},{12,13},{... | collective-permute-start | bytes 50696 | tf_op jit(solution)/shard_map/ppermute | solution.py:152
  120.2 2.1 collective-permute-start.3
  122.4 11.6 %copy.46 = f32[8,8,22,512]{3,1,2,0:T(8,128)} copy(f32[8,8,22,512]{2,1,3,0:T(8,128)} %copy-done.4) | data formatting | bytes 5767168 | tf_op jit(solution)/shard_map/concatenate | solution.py:154
  134.5 0.6 copy.47
  135.1 3.0 %pad_maximum_fusion.1 = f32[8,8,22,518]{3,1,2,0:T(8,128)S(1)} fusion(f32[8,8,22,3]{3,1,2,0:T(8,128)S(1)} %copy.47, f32[8,8,22,512]{3,1,2,0:T(8,128)} %copy.46, f32[8,8,22,3]{3,1,2,0:T(8,128)S(1)} %copy.45), kind=kLoop, calls=%fused_computation.1 | loop fusion | flops 1458688 | bytes 5834752 | tf_op jit(solution)/shard_map/concatenate | solution.py:154
  138.1 1.8 fusion.3
  139.9 1.6 fusion.7
  141.5 0.9 fusion.11
  142.4 4.1 %collective-permute-start.4 = (f32[4,8,3,512]{3,1,2,0:T(8,128)S(1)}, f32[4,8,3,512]{3,1,2,0:T(8,128)S(1)}, u32[]{:S(2)}, u32[]{:S(2)}) collective-permute-start(f32[4,8,3,512]{3,1,2,0:T(8,128)S(1)} %get-tuple-element.16), channel_id=1, source_target_pairs={{0,4},{4,8},{8,12},{12,16},{16,20},{20,24},{24,28},{1,5},{5,9},{9,... | collective-permute-start | bytes 589832 | tf_op jit(solution)/shard_map/ppermute | solution.py:152
  146.5 1.3 collective-permute-start.5
  147.8 5.5 %collective-permute-done.4 = f32[4,8,3,512]{3,1,2,0:T(8,128)S(1)} collective-permute-done((f32[4,8,3,512]{3,1,2,0:T(8,128)S(1)}, f32[4,8,3,512]{3,1,2,0:T(8,128)S(1)}, u32[]{:S(2)}, u32[]{:S(2)}) %collective-permute-start.4) | collective-permute-done | bytes 196640 | tf_op jit(solution)/shard_map/ppermute | solution.py:152
  153.5 4.7 %collective-permute-start.6 = (f32[4,8,22,3]{3,1,2,0:T(8,128)S(1)}, f32[4,8,22,3]{3,1,2,0:T(8,128)S(1)}, u32[]{:S(2)}, u32[]{:S(2)}) collective-permute-start(f32[4,8,22,3]{3,1,2,0:T(8,128)S(1)} %get-tuple-element.12), channel_id=1, source_target_pairs={{0,1},{1,2},{2,3},{4,5},{5,6},{6,7},{8,9},{9,10},{10,11},{12,13},{... | collective-permute-start | bytes 25352 | tf_op jit(solution)/shard_map/ppermute | solution.py:152
  158.2 2.1 %collective-permute-start.7 = (f32[4,8,22,3]{3,1,2,0:T(8,128)S(1)}, f32[4,8,22,3]{3,1,2,0:T(8,128)S(1)}, u32[]{:S(2)}, u32[]{:S(2)}) collective-permute-start(f32[4,8,22,3]{3,1,2,0:T(8,128)S(1)} %get-tuple-element.13), channel_id=1, source_target_pairs={{1,0},{2,1},{3,2},{5,4},{6,5},{7,6},{9,8},{10,9},{11,10},{13,12},{... | collective-permute-start | bytes 25352 | tf_op jit(solution)/shard_map/ppermute | solution.py:153
  160.4 2.2 %collective-permute-done.6 = f32[4,8,22,3]{3,1,2,0:T(8,128)S(1)} collective-permute-done((f32[4,8,22,3]{3,1,2,0:T(8,128)S(1)}, f32[4,8,22,3]{3,1,2,0:T(8,128)S(1)}, u32[]{:S(2)}, u32[]{:S(2)}) %collective-permute-start.6) | collective-permute-done | bytes 8480 | tf_op jit(solution)/shard_map/ppermute | solution.py:152
  162.6 4.4 %collective-permute-done.7 = f32[4,8,22,3]{3,1,2,0:T(8,128)S(1)} collective-permute-done((f32[4,8,22,3]{3,1,2,0:T(8,128)S(1)}, f32[4,8,22,3]{3,1,2,0:T(8,128)S(1)}, u32[]{:S(2)}, u32[]{:S(2)}) %collective-permute-start.7) | collective-permute-done | bytes 8480 | tf_op jit(solution)/shard_map/ppermute | solution.py:153
  167.0 0.6 pad_maximum_fusion.3
  167.6 1.8 fusion.1
  169.4 1.6 fusion.5
  170.9 0.9 fusion.9
  172.7 22.0 %gather.1 = f32[4,64,256]{2,1,0:T(8,128)S(1)} custom-call(f32[4,128,512]{2,1,0:T(8,128)S(1)} %pad_maximum_fusion.5.fields, f32[5,64,256]{2,1,0:T(8,128)S(1)} %bitcast.19), custom_call_target="tpu_custom_call" | custom-call | tf_op jit(solution)/shard_map/gather/pallas_call | solution.py:239
  194.8 0.7 copy.54
  195.5 3.4 %all-to-all-start.1 = ((f32[4,8,8,256]{3,2,0,1:T(8,128)}), f32[4,8,8,256]{3,2,0,1:T(8,128)S(1)}, u32[]{:S(2)}, u32[]{:S(2)}) async-start(f32[4,8,8,256]{3,2,0,1:T(8,128)} %copy.54), calls=%async_computation.1 | async-start | bytes 524288 | tf_op jit(solution)/shard_map/all_to_all | solution.py:248
  198.9 1.0 pad_maximum_fusion.4
  200.0 6.0 %all-to-all-done.1 = f32[4,8,8,256]{3,2,0,1:T(8,128)S(1)} async-done(((f32[4,8,8,256]{3,2,0,1:T(8,128)}), f32[4,8,8,256]{3,2,0,1:T(8,128)S(1)}, u32[]{:S(2)}, u32[]{:S(2)}) %all-to-all-start.1) | async-done | bytes 262176 | tf_op jit(solution)/shard_map/all_to_all | solution.py:248
  206.0 6.1 %unpack.1 = f32[4,1,8192]{2,1,0:T(1,128)} custom-call(f32[4,64,256]{2,1,0:T(8,128)S(1)} %bitcast.21, s32[1,8192]{1,0:T(1,128)S(1)} %get-tuple-element.5.slots), custom_call_target="tpu_custom_call" | custom-call | tf_op jit(solution)/shard_map/unpack/pallas_call | solution.py:251
  (32 shorter events, 2.0 us)
Async XLA Ops:
  1.3 0.9 copy-start
  2.2 0.8 copy-start.1
  2.9 0.8 copy-start.2
  3.7 0.8 copy-start.3
  15.0 14.7 %all-to-all-start = ((f32[5,8,8,256]{3,2,0,1:T(8,128)}), f32[5,8,8,256]{3,2,0,1:T(8,128)S(1)}, u32[]{:S(2)}, u32[]{:S(2)}) async-start(f32[5,8,8,256]{3,2,0,1:T(8,128)} %copy.38), calls=%async_computation | async-start | bytes 655360 | tf_op jit(solution)/shard_map/all_to_all | solution.py:190
  51.3 7.5 %copy-start.5 = (f32[22,518]{1,0:T(8,128)S(1)}, f32[22,518]{1,0:T(8,128)}, u32[]{:S(2)}) copy-start(f32[22,518]{1,0:T(8,128)} %and_convert_fusion) | copy-start | bytes 136756
  52.4 18.1 %collective-permute-start = (f32[8,8,3,512]{3,1,2,0:T(8,128)}, f32[8,8,3,512]{3,1,2,0:T(8,128)}, u32[]{:S(2)}, u32[]{:S(2)}) collective-permute-start(f32[8,8,3,512]{3,1,2,0:T(8,128)} %copy.56), channel_id=1, source_target_pairs={{0,4},{4,8},{8,12},{12,16},{16,20},{20,24},{24,28},{1,5},{5,9},{9,... | collective-permute-start | bytes 1179656 | tf_op jit(solution)/shard_map/ppermute | solution.py:152
  57.5 22.7 %collective-permute-start.1 = (f32[8,8,3,512]{3,1,2,0:T(8,128)}, f32[8,8,3,512]{3,1,2,0:T(8,128)}, u32[]{:S(2)}, u32[]{:S(2)}) collective-permute-start(f32[8,8,3,512]{3,1,2,0:T(8,128)} %copy.57), channel_id=1, source_target_pairs={{4,0},{8,4},{12,8},{16,12},{20,16},{24,20},{28,24},{5,1},{9,5},{13... | collective-permute-start | bytes 1179656 | tf_op jit(solution)/shard_map/ppermute | solution.py:153
  89.8 32.5 %copy-start.6 = (f32[22,518]{1,0:T(8,128)S(1)}, f32[22,518]{1,0:T(8,128)}, u32[]{:S(2)}) copy-start(f32[22,518]{1,0:T(8,128)} %and_convert_fusion) | copy-start | bytes 136756
  107.7 5.7 %copy-start.4 = (f32[8,8,22,512]{2,1,3,0:T(8,128)}, f32[8,8,22,512]{2,1,3,0:T(8,128)S(1)}, u32[]{:S(2)}) copy-start(f32[8,8,22,512]{2,1,3,0:T(8,128)S(1)} %pad_maximum_fusion) | copy-start | bytes 8650756
  113.4 20.6 %collective-permute-start.2 = (f32[8,8,22,3]{2,1,3,0:T(8,128)S(1)}, f32[8,8,22,3]{2,1,3,0:T(8,128)S(1)}, u32[]{:S(2)}, u32[]{:S(2)}) collective-permute-start(f32[8,8,22,3]{2,1,3,0:T(8,128)S(1)} %get-tuple-element.8), channel_id=1, source_target_pairs={{0,1},{1,2},{2,3},{4,5},{5,6},{6,7},{8,9},{9,10},{10,11},{12,13},{... | collective-permute-start | bytes 50696 | tf_op jit(solution)/shard_map/ppermute | solution.py:152
  120.2 14.4 %collective-permute-start.3 = (f32[8,8,22,3]{2,1,3,0:T(8,128)S(1)}, f32[8,8,22,3]{2,1,3,0:T(8,128)S(1)}, u32[]{:S(2)}, u32[]{:S(2)}) collective-permute-start(f32[8,8,22,3]{2,1,3,0:T(8,128)S(1)} %get-tuple-element.9), channel_id=1, source_target_pairs={{1,0},{2,1},{3,2},{5,4},{6,5},{7,6},{9,8},{10,9},{11,10},{13,12},{... | collective-permute-start | bytes 50696 | tf_op jit(solution)/shard_map/ppermute | solution.py:153
  135.1 3.0 %copy-start.8 = (f32[20,516]{1,0:T(8,128)S(1)}, f32[20,516]{1,0:T(8,128)}, u32[]{:S(2)}) copy-start(f32[20,516]{1,0:T(8,128)} %slice_multiply_fusion.1) | copy-start | bytes 123844
  138.1 1.8 copy-start.7
  142.4 10.9 %collective-permute-start.4 = (f32[4,8,3,512]{3,1,2,0:T(8,128)S(1)}, f32[4,8,3,512]{3,1,2,0:T(8,128)S(1)}, u32[]{:S(2)}, u32[]{:S(2)}) collective-permute-start(f32[4,8,3,512]{3,1,2,0:T(8,128)S(1)} %get-tuple-element.16), channel_id=1, source_target_pairs={{0,4},{4,8},{8,12},{12,16},{16,20},{20,24},{24,28},{1,5},{5,9},{9,... | collective-permute-start | bytes 589832 | tf_op jit(solution)/shard_map/ppermute | solution.py:152
  146.5 6.8 %collective-permute-start.5 = (f32[4,8,3,512]{3,1,2,0:T(8,128)S(1)}, f32[4,8,3,512]{3,1,2,0:T(8,128)S(1)}, u32[]{:S(2)}, u32[]{:S(2)}) collective-permute-start(f32[4,8,3,512]{3,1,2,0:T(8,128)S(1)} %get-tuple-element.17), channel_id=1, source_target_pairs={{4,0},{8,4},{12,8},{16,12},{20,16},{24,20},{28,24},{5,1},{9,5},{13... | collective-permute-start | bytes 589832 | tf_op jit(solution)/shard_map/ppermute | solution.py:153
  153.5 9.0 %collective-permute-start.6 = (f32[4,8,22,3]{3,1,2,0:T(8,128)S(1)}, f32[4,8,22,3]{3,1,2,0:T(8,128)S(1)}, u32[]{:S(2)}, u32[]{:S(2)}) collective-permute-start(f32[4,8,22,3]{3,1,2,0:T(8,128)S(1)} %get-tuple-element.12), channel_id=1, source_target_pairs={{0,1},{1,2},{2,3},{4,5},{5,6},{6,7},{8,9},{9,10},{10,11},{12,13},{... | collective-permute-start | bytes 25352 | tf_op jit(solution)/shard_map/ppermute | solution.py:152
  158.2 8.7 %collective-permute-start.7 = (f32[4,8,22,3]{3,1,2,0:T(8,128)S(1)}, f32[4,8,22,3]{3,1,2,0:T(8,128)S(1)}, u32[]{:S(2)}, u32[]{:S(2)}) collective-permute-start(f32[4,8,22,3]{3,1,2,0:T(8,128)S(1)} %get-tuple-element.13), channel_id=1, source_target_pairs={{1,0},{2,1},{3,2},{5,4},{6,5},{7,6},{9,8},{10,9},{11,10},{13,12},{... | collective-permute-start | bytes 25352 | tf_op jit(solution)/shard_map/ppermute | solution.py:153
  195.5 10.4 %all-to-all-start.1 = ((f32[4,8,8,256]{3,2,0,1:T(8,128)}), f32[4,8,8,256]{3,2,0,1:T(8,128)S(1)}, u32[]{:S(2)}, u32[]{:S(2)}) async-start(f32[4,8,8,256]{3,2,0,1:T(8,128)} %copy.54), calls=%async_computation.1 | async-start | bytes 524288 | tf_op jit(solution)/shard_map/all_to_all | solution.py:248

commit v2 on v1

--- a/solution.py
+++ b/solution.py
@@ -84,7 +84,13 @@
     lax.fori_loop(0, part_rows // block, step, jnp.zeros((span, 1), F32))
 
 
-def deposit_kernel(group, recv, out):
+def x_major(ids, layers, width_x, cols):
+    line = lax.shift_right_arithmetic(ids, int(math.log2(cols)))
+    layer = lax.shift_right_arithmetic(line, int(math.log2(width_x)))
+    return lax.bitwise_and(line, width_x - 1) * layers + layer
+
+
+def deposit_kernel(group, layers, recv, out):
     comps, rows, cols = out.shape
     out[...] = jnp.zeros_like(out)
 
@@ -95,7 +101,7 @@
             jnp.concatenate([b[j : j + 1] for j in range(group)], axis=1) for b in block
         ]
         ids = flat[0].astype(jnp.int32)
-        row = lax.shift_right_arithmetic(ids, int(math.log2(cols)))
+        row = x_major(ids, layers, rows // layers, cols)
         col = lax.bitwise_and(ids, cols - 1)
         out[...] += spread(flat[1:], row, col, rows, cols).reshape(out.shape)
         return carry
@@ -104,10 +110,16 @@
     out[0] = jnp.minimum(out[0], PHI_LIMIT)
 
 
-def gather_kernel(group, fields, ids_ref, out, high, low):
-    comps, rows, cols = fields.shape
-    table = fields[...].reshape(comps * rows, cols)
-    high[...], low[...] = two_parts(table)
+def gather_kernel(group, smooth, ids_ref, fields, out, high, low):
+    comps, width_x, layers, cols = smooth.shape
+    rows = width_x * layers
+    for x in range(width_x):
+        void = 1.0 - smooth[0, x]
+        for c in range(comps):
+            value = void if c == 0 else -smooth[c, x] / void
+            fields[c, :, x, :] = value
+            lines = pl.ds(c * rows + x * layers, layers)
+            high[lines], low[lines] = two_parts(value)
 
     def step(g, carry):
         lines = pl.ds(pl.multiple_of(g * group, group), group)
@@ -115,7 +127,7 @@
         found = []
         for j in range(group):
             ids = block[j : j + 1]
-            row = lax.shift_right_arithmetic(ids, int(math.log2(cols)))
+            row = x_major(ids, layers, width_x, cols)
             col = lax.bitwise_and(ids, cols - 1)
             found.append(pick(high[...], low[...], row, col, rows, cols))
         for c in range(comps):
@@ -142,23 +154,153 @@
     lax.fori_loop(0, slots.shape[1] // block, step, 0)
 
 
-def padded_2(array, sides, width):
-    for axis, dim in sides:
-        count, length = (lax.axis_size(axis), array.shape[dim])
-        up = [(i, (i + 1) % count) for i in range(count - 1)]
-        down = [(j, i) for i, j in up]
-        last = lax.slice_in_dim(array, length - width, length, axis=dim)
-        first = lax.slice_in_dim(array, 0, width, axis=dim)
-        before = lax.ppermute(last, axis, up)
-        after = lax.ppermute(first, axis, down)
-        array = jnp.concatenate([before, array, after], axis=dim)
-    return array
-
-
-def relax_once(source, padded):
-    beside = padded[:, :, 2:, 1:-1] + padded[:, :, :-2, 1:-1]
-    beside = beside + padded[:, :, 1:-1, 2:] + padded[:, :, 1:-1, :-2]
-    return (source + NU_WEIGHT * beside) / (1.0 + 4.0 * NU_WEIGHT)
+MESH = pl.DeviceIdType.MESH
+NEAR = [(dx, dy) for dx in (-1, 0, 1) for dy in (-1, 0, 1) if (dx, dy) != (0, 0)]
+
+
+def sweeps_kernel(rim, solid, drag, target, out, smooth, source, ysend, yrecv, send_sem, recv_sem):
+    comps, width_x, layers, width_y = target.shape
+    span, depth = lax.axis_index("span"), lax.axis_index("depth")
+    span_size, depth_size = lax.axis_size("span"), lax.axis_size("depth")
+    own = pl.ds(128, width_y)
+    total_x = width_x + 2 * rim
+
+    def has(dx, dy):
+        x, y = span + dx, depth + dy
+        return (x >= 0) & (x < span_size) & (y >= 0) & (y < depth_size)
+
+    barrier = pltpu.get_barrier_semaphore()
+    for dx, dy in NEAR:
+
+        @pl.when(has(dx, dy))
+        def _(dx=dx, dy=dy):
+            pl.semaphore_signal(
+                barrier, inc=1, device_id=(span + dx, depth + dy), device_id_type=MESH
+            )
+
+    buffers = (smooth, source)
+
+    def copy_of(which, at):
+        dx, dy = NEAR[at]
+        width = rim - which
+        buffer = buffers[which]
+        if dy == 0 and dx == 1:
+            src = buffer.at[:, pl.ds(width_x + rim - width, width), :, own]
+            dst = buffer.at[:, pl.ds(rim - width, width), :, own]
+        elif dy == 0:
+            src = buffer.at[:, pl.ds(rim, width), :, own]
+            dst = buffer.at[:, pl.ds(width_x + rim, width), :, own]
+        else:
+            side = (dy + 1) // 2
+            src = ysend.at[which, side]
+            dst = yrecv.at[which, side, dx + 1]
+        return pltpu.make_async_remote_copy(
+            src_ref=src,
+            dst_ref=dst,
+            send_sem=send_sem.at[which, at],
+            recv_sem=recv_sem.at[which, at],
+            device_id=(span + dx, depth + dy),
+            device_id_type=MESH,
+        )
+
+    def fill_own(which, row_of):
+        buffer = buffers[which]
+        for c in range(comps):
+            for x in range(width_x):
+                buffer[c, rim + x, :, own] = row_of(c, x)
+            for side, start in ((0, 128), (1, width_y)):
+                edge = buffer[c, pl.ds(rim, width_x), :, pl.ds(start, 128)]
+                turned = edge.reshape(width_x * layers, 128).T
+                ysend[which, side, c] = turned[:8] if side == 0 else turned[120:]
+
+    def edges_zero(which):
+        buffer = buffers[which]
+        for dx, start in ((1, 0), (-1, width_x + rim)):
+
+            @pl.when(jnp.logical_not(has(-dx, 0)))
+            def _(start=start):
+                buffer[:, pl.ds(start, rim), :, own] = jnp.zeros(
+                    (comps, rim, layers, width_y), F32
+                )
+
+    fill_own(0, lambda c, x: solid[:, x, :] if c == 0 else drag[c - 1, :, x, :])
+    edges_zero(0)
+    edges_zero(1)
+    count = sum(has(dx, dy).astype(jnp.int32) for dx, dy in NEAR)
+    pl.semaphore_wait(barrier, count)
+    for which in range(2):
+        if which == 1:
+            fill_own(1, lambda c, x: target[c, x])
+        for at, (dx, dy) in enumerate(NEAR):
+
+            @pl.when(has(dx, dy))
+            def _(at=at, which=which):
+                copy_of(which, at).start()
+
+    def pads(which):
+        buffer = buffers[which]
+        for at, (dx, dy) in enumerate(NEAR):
+            if dy == 0:
+
+                @pl.when(has(-dx, 0))
+                def _(at=at):
+                    copy_of(which, at).wait_recv()
+
+                continue
+            side = (dy + 1) // 2
+            lanes = pl.ds(128 + width_y, 128) if side == 0 else pl.ds(0, 128)
+            if dx == 0:
+                rows, taken = pl.ds(rim, width_x), slice(0, width_x)
+            elif dx == 1:
+                rows, taken = pl.ds(0, rim), slice(width_x - rim, width_x)
+            else:
+                rows, taken = pl.ds(width_x + rim, rim), slice(0, rim)
+
+            @pl.when(has(-dx, -dy))
+            def _(at=at, side=side, lanes=lanes, rows=rows, taken=taken, dx=dx):
+                copy_of(which, at).wait_recv()
+                for c in range(comps):
+                    block = yrecv[which, side, dx + 1, c]
+                    rest = jnp.zeros((120, 128), F32)
+                    parts = [block, rest] if side == 0 else [rest, block]
+                    turned = jnp.concatenate(parts, axis=0).T.reshape(width_x, layers, 128)
+                    buffer[c, rows, :, lanes] = turned[taken]
+
+            @pl.when(jnp.logical_not(has(-dx, -dy)))
+            def _(lanes=lanes, rows=rows, taken=taken):
+                n = taken.stop - taken.start
+                buffer[:, rows, :, lanes] = jnp.zeros((comps, n, layers, 128), F32)
+
+    def sent(which):
+        for at, (dx, dy) in enumerate(NEAR):
+
+            @pl.when(has(dx, dy))
+            def _(at=at):
+                copy_of(which, at).wait_send()
+
+    pads(0)
+    pads(1)
+    sent(0)
+    lane = lax.broadcasted_iota(jnp.int32, (layers, width_y + 256), 1)
+    first = jnp.where(depth > 0, 0, 128)
+    end = jnp.where(depth < depth_size - 1, width_y + 256, width_y + 128)
+    scale = jnp.where((lane >= first) & (lane < end), 1.0 / (1.0 + 4.0 * NU_WEIGHT), 0.0)
+    first_row = jnp.where(span > 0, 0, rim)
+    end_row = jnp.where(span < span_size - 1, total_x, width_x + rim)
+    for c in range(comps):
+        for sweep in range(1, SWEEPS + 1):
+
+            def row_step(x, before, c=c):
+                here = smooth[c, x]
+                beside = before + smooth[c, x + 1]
+                beside = beside + pltpu.roll(here, 1, 1) + pltpu.roll(here, width_y + 255, 1)
+                inside = jnp.where((x >= first_row) & (x < end_row), 1.0, 0.0)
+                smooth[c, x] = (source[c, x] + NU_WEIGHT * beside) * (scale * inside)
+                return here
+
+            lax.fori_loop(sweep, total_x - sweep, row_step, smooth[c, sweep - 1], unroll=2)
+        out[c] = smooth[c, pl.ds(rim, width_x), :, own]
+    sent(1)
 
 
 VMEM = pl.BlockSpec(memory_space=pltpu.VMEM)
@@ -168,7 +310,6 @@
 
 def on_device(part_slab, part_cell, part_volume, part_drag, part_count, prior_solid, prior_drag):
     span_size = lax.axis_size("span")
-    depth_size = lax.axis_size("depth")
     part_rows = part_cell.shape[1]
     cap = 2 * part_rows // span_size
     layers, width_x, width_y = prior_solid.shape
@@ -192,59 +333,46 @@
     ).reshape(5, lines, cols)
     grid_rows = layers * width_x
     target = pl.pallas_call(
-        functools.partial(deposit_kernel, 8),
+        functools.partial(deposit_kernel, 8, layers),
         out_shape=jax.ShapeDtypeStruct((4, grid_rows, width_y), F32),
         in_specs=[VMEM],
         out_specs=VMEM,
         compiler_params=LIMIT,
         name="deposit",
     )(recv)
-    target = target.reshape(4, layers, width_x, width_y)
-    smooth = jnp.concatenate([prior_solid[None], prior_drag], axis=0)
-    rim_width = 3
-    row_ids = (
-        lax.axis_index("span") * width_x
-        - rim_width
-        + jnp.arange(width_x + 2 * rim_width, dtype=jnp.int32)
-    )
-    col_ids = (
-        lax.axis_index("depth") * width_y
-        - rim_width
-        + jnp.arange(width_y + 2 * rim_width, dtype=jnp.int32)
-    )
-    row_inside = (row_ids >= 0) & (row_ids < span_size * width_x)
-    col_inside = (col_ids >= 0) & (col_ids < depth_size * width_y)
-    inside = (row_inside[:, None] & col_inside[None, :]).astype(jnp.float32)
-    stacked = padded_2(
-        jnp.concatenate([smooth, target], axis=0), (("span", 2), ("depth", 3)), rim_width
-    )
-    padded = stacked[:4]
-    target_wide = stacked[4:]
-    for round_index in range(SWEEPS // rim_width):
-        if round_index > 0:
-            padded = padded_2(smooth, (("span", 2), ("depth", 3)), rim_width)
-        for inner_step in range(rim_width):
-            edge_offset = inner_step + 1
-            size_x = width_x + 2 * (rim_width - edge_offset)
-            size_y = width_y + 2 * (rim_width - edge_offset)
-            region = target_wide[
-                :, :, edge_offset : edge_offset + size_x, edge_offset : edge_offset + size_y
-            ]
-            keeper = inside[edge_offset : edge_offset + size_x, edge_offset : edge_offset + size_y]
-            padded = relax_once(region, padded) * keeper[None, None]
-        smooth = padded
-    void_fraction = 1.0 - smooth[0]
-    fields = jnp.concatenate([void_fraction[None], -smooth[1:] / void_fraction[None]], axis=0)
-    table = fields.reshape(4, grid_rows, width_y)
-    values = pl.pallas_call(
+    target = target.reshape(4, width_x, layers, width_y)
+    rim = SWEEPS
+    wide = (4, width_x + 2 * rim, layers, width_y + 256)
+    smooth = pl.pallas_call(
+        functools.partial(sweeps_kernel, rim),
+        out_shape=jax.ShapeDtypeStruct(target.shape, F32),
+        in_specs=[VMEM] * 3,
+        out_specs=VMEM,
+        scratch_shapes=[
+            pltpu.VMEM(wide, F32),
+            pltpu.VMEM(wide, F32),
+            pltpu.VMEM((2, 2, 4, 8, 128), F32),
+            pltpu.VMEM((2, 2, 3, 4, 8, 128), F32),
+            pltpu.SemaphoreType.DMA((2, 8)),
+            pltpu.SemaphoreType.DMA((2, 8)),
+        ],
+        compiler_params=pltpu.CompilerParams(
+            vmem_limit_bytes=48 * 1024 * 1024, collective_id=0, has_side_effects=True
+        ),
+        name="sweeps",
+    )(prior_solid, prior_drag, target)
+    fields, values = pl.pallas_call(
         functools.partial(gather_kernel, 8),
-        out_shape=jax.ShapeDtypeStruct((4, lines, cols), F32),
+        out_shape=(
+            jax.ShapeDtypeStruct((4, layers, width_x, width_y), F32),
+            jax.ShapeDtypeStruct((4, lines, cols), F32),
+        ),
         in_specs=[VMEM] * 2,
-        out_specs=VMEM,
+        out_specs=(VMEM, VMEM),
         scratch_shapes=[pltpu.VMEM((4 * grid_rows, width_y), BF)] * 2,
         compiler_params=LIMIT,
         name="gather",
-    )(table, recv)
+    )(smooth, recv)
     returned = lax.all_to_all(
         values.reshape(4, span_size, per, cols), "span", split_axis=1, concat_axis=1, tiled=True
     ).reshape(4, lines, cols)

time: 213 us -> 155 us (0.73)
  Pallas kernels: 58 us -> 114 us
  local copies, waits for them, and re-layouts: 53.7 us -> 3.25 us
  starting transfers between devices: 36.3 us -> 0 us
  blocking collectives: 0 us -> 35.5 us
  other arithmetic: 35.1 us -> 0 us
  waiting for transfers between devices: 27.3 us -> 0 us
    pallas_call x2 -> x3, Pallas kernels: 42.1 us -> 97.6 us  [the longest x1 54.9 us: on_device(): pl.pallas_call(functools.partial(sweeps_kernel, rim), out_shape=jax.Shape...]
    all_to_all x0 -> x2, blocking collectives: none -> 35.5 us  [the longest x1 20.3 us: on_device(): lax.all_to_all(values.reshape(4, span_size, per, cols), 'span', split_axi...]
    ppermute x8 -> x0, starting transfers between devices: 26.5 us -> none  [the longest x4 19.7 us: padded_2(): before = lax.ppermute(last, axis, up)]
    concatenate x6 -> x0, other arithmetic: 24.1 us -> none  [the longest x3 21.5 us: padded_2(): array = jnp.concatenate([before, array, after], axis=dim)]
    ppermute x4 -> x0, local copies, waits for them, and re-layouts: 20.4 us -> none  [the longest x2 10.2 us: padded_2(): before = lax.ppermute(last, axis, up)]
    concatenate x2 -> x0, local copies, waits for them, and re-layouts: 20.2 us -> none  [the longest x1 11.6 us: padded_2(): array = jnp.concatenate([before, array, after], axis=dim)]
    ppermute x8 -> x0, waiting for transfers between devices: 13.8 us -> none  [the longest x4 9.37 us: padded_2(): before = lax.ppermute(last, axis, up)]
    all_to_all x2 -> x0, waiting for transfers between devices: 13.5 us -> none  [the longest x1 7.57 us: on_device(): lax.all_to_all(packed.reshape(5, span_size, per, cols), 'span', split_axi...]
  transfers between devices with their start and end apart: 10 -> 0, of which waited for: 6 -> 0; matrix products, arithmetic and copies ran while one was open for 16% -> 0% of each run, Pallas kernels for 0% -> 0%
where the time goes in v2:
time: 155 us; the launch traced here: 154 us
  Pallas kernels  114 us (74%)
  blocking collectives  35.5 us (23%)
  local copies, waits for them, and re-layouts  3.25 us (2%)
    pallas_call x1, Pallas kernels, on_device(): pl.pallas_call(functools.partial(sweeps_kernel, rim), out_shape=jax.Shape...  54.9 us
    pallas_call x1, Pallas kernels, on_device(): pl.pallas_call(functools.partial(gather_kernel, 8), out_shape=(jax.ShapeD...  22.4 us
    all_to_all x1, blocking collectives, on_device(): lax.all_to_all(values.reshape(4, span_size, per, cols), 'span', split_axi...  20.3 us
    pallas_call x1, Pallas kernels, on_device(): pl.pallas_call(functools.partial(deposit_kernel, 8, layers), out_shape=ja...  20.3 us
    all_to_all x1, blocking collectives, on_device(): lax.all_to_all(packed.reshape(5, span_size, per, cols), 'span', split_axi...  15.2 us
    pallas_call x1, Pallas kernels, on_device(): pl.pallas_call(functools.partial(pack_kernel, span_size, cap, block), out...  9.78 us
    pallas_call x1, Pallas kernels, on_device(): pl.pallas_call(functools.partial(unpack_kernel, block), out_shape=jax.Sha...  6.1 us
    unnamed x12, local copies, waits for them, and re-layouts  3.17 us

profile of v2, /device:TPU:1, one launch (start us, length us, event | category | flops | bytes accessed | tf_op | source)
XLA Modules:
  0.0 153.6 jit_solution(5139390031905757238)
XLA Ops:
  1.3 0.0 copy-start.2
  1.3 0.9 copy-done.2
  2.2 0.0 copy-start.3
  2.2 0.8 copy-done.3
  2.9 0.0 copy-start.4
  2.9 0.8 copy-done.4
  3.7 0.0 copy-start.5
  3.7 0.8 copy-done.5
  4.4 9.8 %pack.1 = (f32[5,64,256]{2,1,0:T(8,128)S(1)}, s32[1,8192]{1,0:T(1,128)S(1)}) custom-call(s32[1,1]{1,0:T(1,128)S(6)} %copy.17.count, s32[1,8192]{1,0:T(1,128)S(1)} %bitcast.16, s32[1,8192]{1,0:T(1,128)S(1)} %copy-done.4, f32[1,8192]{1,0:T(1,128)S(1)} %copy-done.5, f32[3,1,8192]{2,1,0:T(1,128)S(1)} %copy-done.2), custom_call_target="tpu_custom_call" | custom-call | tf_op jit(solution)/shard_map/pack/pallas_call | solution.py:319
  14.3 15.2 %all_to_all.10 = f32[5,8,8,256]{3,2,0,1:T(8,128)S(1)} all-to-all(f32[5,8,8,256]{3,2,0,1:T(8,128)S(1)} %copy.9), channel_id=1, replica_groups=mesh['span'=8,'depth'=4] {'span'}, dimensions={1} | all-to-all | bytes 655360 | tf_op jit(solution)/shard_map/all_to_all | solution.py:331
  29.5 0.0 copy-start
  29.5 0.0 copy-start.1
  29.5 20.3 %deposit.1 = f32[4,128,512]{2,1,0:T(8,128)S(1)} custom-call(f32[5,64,256]{2,1,0:T(8,128)S(1)} %bitcast.11), custom_call_target="tpu_custom_call" | custom-call | tf_op jit(solution)/shard_map/deposit/pallas_call | solution.py:335
  49.8 0.0 copy-done
  49.8 0.0 copy-done.1
  49.8 54.9 %sweeps.1.smooth = f32[4,16,8,512]{3,2,1,0:T(8,128)S(1)} custom-call(f32[8,16,512]{2,1,0:T(8,128)S(1)} %copy-done.1, f32[3,8,16,512]{3,2,1,0:T(8,128)S(1)} %copy-done, f32[4,16,8,512]{3,2,1,0:T(8,128)S(1)} %bitcast.10), custom_call_target="tpu_custom_call" | custom-call | tf_op jit(solution)/shard_map/sweeps/pallas_call | solution.py:346
  104.7 22.4 %gather.1 = (f32[4,8,16,512]{3,2,1,0:T(8,128)}, f32[4,64,256]{2,1,0:T(8,128)S(1)}) custom-call(f32[4,16,8,512]{3,2,1,0:T(8,128)S(1)} %sweeps.1.smooth, f32[5,64,256]{2,1,0:T(8,128)S(1)} %bitcast.12), custom_call_target="tpu_custom_call" | custom-call | tf_op jit(solution)/shard_map/gather/pallas_call | solution.py:364
  127.2 20.3 %all_to_all.11 = f32[4,8,8,256]{3,2,0,1:T(8,128)S(1)} all-to-all(f32[4,8,8,256]{3,2,0,1:T(8,128)S(1)} %copy.11), channel_id=1, replica_groups=mesh['span'=8,'depth'=4] {'span'}, dimensions={1} | all-to-all | bytes 524288 | tf_op jit(solution)/shard_map/all_to_all | solution.py:376
  147.5 6.1 %unpack.1 = f32[4,1,8192]{2,1,0:T(1,128)} custom-call(f32[4,64,256]{2,1,0:T(8,128)S(1)} %bitcast.13, s32[1,8192]{1,0:T(1,128)S(1)} %get-tuple-element.9.slots), custom_call_target="tpu_custom_call" | custom-call | tf_op jit(solution)/shard_map/unpack/pallas_call | solution.py:379
  (4 shorter events, 0.1 us)
Async XLA Ops:
  1.3 0.9 copy-start.2
  2.2 0.8 copy-start.3
  2.9 0.8 copy-start.4
  3.7 0.8 copy-start.5
  29.5 20.3 %copy-start = (f32[3,8,16,512]{3,2,1,0:T(8,128)S(1)}, f32[3,8,16,512]{3,2,1,0:T(8,128)}, u32[]{:S(2)}) copy-start(f32[3,8,16,512]{3,2,1,0:T(8,128)} %drag.3) | copy-start | bytes 2359300
  29.5 20.3 %copy-start.1 = (f32[8,16,512]{2,1,0:T(8,128)S(1)}, f32[8,16,512]{2,1,0:T(8,128)}, u32[]{:S(2)}) copy-start(f32[8,16,512]{2,1,0:T(8,128)} %solid.1) | copy-start | bytes 786436

commit v3 on v2

--- a/solution.py
+++ b/solution.py
@@ -158,7 +158,56 @@
 NEAR = [(dx, dy) for dx in (-1, 0, 1) for dy in (-1, 0, 1) if (dx, dy) != (0, 0)]
 
 
-def sweeps_kernel(rim, solid, drag, target, out, smooth, source, ysend, yrecv, send_sem, recv_sem):
+def exchange_kernel(count, data, out, send_sem, recv_sem, own_sem):
+    span, depth = lax.axis_index("span"), lax.axis_index("depth")
+    barrier = pltpu.get_barrier_semaphore()
+    for k in range(1, count):
+        to = lax.rem(span + k, count)
+        pl.semaphore_signal(barrier, inc=1, device_id=(to, depth), device_id_type=MESH)
+    own = pltpu.make_async_copy(data.at[:, span], out.at[:, span], own_sem)
+    own.start()
+    pl.semaphore_wait(barrier, count - 1)
+    copies = []
+    for k in range(1, count):
+        to = lax.rem(span + k, count)
+        copies.append(
+            pltpu.make_async_remote_copy(
+                src_ref=data.at[:, to],
+                dst_ref=out.at[:, span],
+                send_sem=send_sem.at[k],
+                recv_sem=recv_sem.at[k],
+                device_id=(to, depth),
+                device_id_type=MESH,
+            )
+        )
+        copies[-1].start()
+    own.wait()
+    for copy in copies:
+        copy.wait()
+
+
+def exchange(data, number):
+    count = data.shape[1]
+    return pl.pallas_call(
+        functools.partial(exchange_kernel, count),
+        out_shape=jax.ShapeDtypeStruct(data.shape, F32),
+        in_specs=[VMEM],
+        out_specs=VMEM,
+        scratch_shapes=[
+            pltpu.SemaphoreType.DMA((count,)),
+            pltpu.SemaphoreType.DMA((count,)),
+            pltpu.SemaphoreType.DMA,
+        ],
+        compiler_params=pltpu.CompilerParams(
+            vmem_limit_bytes=16 * 1024 * 1024, collective_id=number, has_side_effects=True
+        ),
+        name=f"exchange_{number}",
+    )(data)
+
+
+def sweeps_kernel(
+    rim, solid, drag, above, below, target, out, smooth, source, ysend, yrecv, send_sem, recv_sem
+):
     comps, width_x, layers, width_y = target.shape
     span, depth = lax.axis_index("span"), lax.axis_index("depth")
     span_size, depth_size = lax.axis_size("span"), lax.axis_size("depth")
@@ -180,71 +229,72 @@
 
     buffers = (smooth, source)
 
-    def copy_of(which, at):
+    def copy_of(c, which, at):
         dx, dy = NEAR[at]
         width = rim - which
         buffer = buffers[which]
         if dy == 0 and dx == 1:
-            src = buffer.at[:, pl.ds(width_x + rim - width, width), :, own]
-            dst = buffer.at[:, pl.ds(rim - width, width), :, own]
+            src = buffer.at[c, pl.ds(width_x + rim - width, width), :, own]
+            dst = buffer.at[c, pl.ds(rim - width, width), :, own]
         elif dy == 0:
-            src = buffer.at[:, pl.ds(rim, width), :, own]
-            dst = buffer.at[:, pl.ds(width_x + rim, width), :, own]
+            src = buffer.at[c, pl.ds(rim, width), :, own]
+            dst = buffer.at[c, pl.ds(width_x + rim, width), :, own]
         else:
             side = (dy + 1) // 2
-            src = ysend.at[which, side]
-            dst = yrecv.at[which, side, dx + 1]
+            src = ysend.at[which, side, c]
+            dst = yrecv.at[which, side, dx + 1, c]
         return pltpu.make_async_remote_copy(
             src_ref=src,
             dst_ref=dst,
-            send_sem=send_sem.at[which, at],
-            recv_sem=recv_sem.at[which, at],
+            send_sem=send_sem.at[c, which, at],
+            recv_sem=recv_sem.at[c, which, at],
             device_id=(span + dx, depth + dy),
             device_id_type=MESH,
         )
 
-    def fill_own(which, row_of):
+    def sides(which):
+        return [(at, d) for at, d in enumerate(NEAR) if which == 1 or d[1] != 0]
+
+    def fill_own(c, which, row_of):
         buffer = buffers[which]
-        for c in range(comps):
-            for x in range(width_x):
-                buffer[c, rim + x, :, own] = row_of(c, x)
-            for side, start in ((0, 128), (1, width_y)):
-                edge = buffer[c, pl.ds(rim, width_x), :, pl.ds(start, 128)]
-                turned = edge.reshape(width_x * layers, 128).T
-                ysend[which, side, c] = turned[:8] if side == 0 else turned[120:]
-
-    def edges_zero(which):
-        buffer = buffers[which]
-        for dx, start in ((1, 0), (-1, width_x + rim)):
-
-            @pl.when(jnp.logical_not(has(-dx, 0)))
-            def _(start=start):
-                buffer[:, pl.ds(start, rim), :, own] = jnp.zeros(
-                    (comps, rim, layers, width_y), F32
-                )
-
-    fill_own(0, lambda c, x: solid[:, x, :] if c == 0 else drag[c - 1, :, x, :])
-    edges_zero(0)
-    edges_zero(1)
+        for x in range(width_x):
+            buffer[c, rim + x, :, own] = row_of(x)
+        for side, start in ((0, 128), (1, width_y)):
+            edge = buffer[c, pl.ds(rim, width_x), :, pl.ds(start, 128)]
+            turned = edge.reshape(width_x * layers, 128).T
+            ysend[which, side, c] = turned[:8] if side == 0 else turned[120:]
+
+    for c in range(comps):
+        fill_own(c, 1, lambda x: target[c, x])
+        fill_own(c, 0, lambda x: solid[:, x, :] if c == 0 else drag[c - 1, :, x, :])
     count = sum(has(dx, dy).astype(jnp.int32) for dx, dy in NEAR)
     pl.semaphore_wait(barrier, count)
-    for which in range(2):
-        if which == 1:
-            fill_own(1, lambda c, x: target[c, x])
-        for at, (dx, dy) in enumerate(NEAR):
-
-            @pl.when(has(dx, dy))
-            def _(at=at, which=which):
-                copy_of(which, at).start()
-
-    def pads(which):
+    for c in range(comps):
+        for which in range(2):
+            for at, (dx, dy) in sides(which):
+
+                @pl.when(has(dx, dy))
+                def _(c=c, at=at, which=which):
+                    copy_of(c, which, at).start()
+
+    for c in range(comps):
+        for r in range(rim):
+            smooth[c, r, :, own] = above[c, :, r, :]
+            smooth[c, width_x + rim + r, :, own] = below[c, :, r, :]
+    for dx, start in ((1, 0), (-1, width_x + rim)):
+
+        @pl.when(jnp.logical_not(has(-dx, 0)))
+        def _(start=start):
+            source[:, pl.ds(start, rim), :, own] = jnp.zeros((comps, rim, layers, width_y), F32)
+
+    def pads(c, which):
         buffer = buffers[which]
-        for at, (dx, dy) in enumerate(NEAR):
+        for at, (dx, dy) in sides(which):
             if dy == 0:
 
                 @pl.when(has(-dx, 0))
                 def _(at=at):
-                    copy_of(which, at).wait_recv()
+                    copy_of(c, which, at).wait_recv()
 
                 continue
             side = (dy + 1) // 2
@@ -258,29 +308,25 @@
 
             @pl.when(has(-dx, -dy))
             def _(at=at, side=side, lanes=lanes, rows=rows, taken=taken, dx=dx):
-                copy_of(which, at).wait_recv()
-                for c in range(comps):
-                    block = yrecv[which, side, dx + 1, c]
-                    rest = jnp.zeros((120, 128), F32)
-                    parts = [block, rest] if side == 0 else [rest, block]
-                    turned = jnp.concatenate(parts, axis=0).T.reshape(width_x, layers, 128)
-                    buffer[c, rows, :, lanes] = turned[taken]
+                copy_of(c, which, at).wait_recv()
+                block = yrecv[which, side, dx + 1, c]
+                rest = jnp.zeros((120, 128), F32)
+                parts = [block, rest] if side == 0 else [rest, block]
+                turned = jnp.concatenate(parts, axis=0).T.reshape(width_x, layers, 128)
+                buffer[c, rows, :, lanes] = turned[taken]
 
             @pl.when(jnp.logical_not(has(-dx, -dy)))
             def _(lanes=lanes, rows=rows, taken=taken):
                 n = taken.stop - taken.start
-                buffer[:, rows, :, lanes] = jnp.zeros((comps, n, layers, 128), F32)
-
-    def sent(which):
-        for at, (dx, dy) in enumerate(NEAR):
+                buffer[c, rows, :, lanes] = jnp.zeros((n, layers, 128), F32)
+
+    def sent(c, which):
+        for at, (dx, dy) in sides(which):
 
             @pl.when(has(dx, dy))
             def _(at=at):
-                copy_of(which, at).wait_send()
-
-    pads(0)
-    pads(1)
-    sent(0)
+                copy_of(c, which, at).wait_send()
+
     lane = lax.broadcasted_iota(jnp.int32, (layers, width_y + 256), 1)
     first = jnp.where(depth > 0, 0, 128)
     end = jnp.where(depth < depth_size - 1, width_y + 256, width_y + 128)
@@ -288,6 +334,8 @@
     first_row = jnp.where(span > 0, 0, rim)
     end_row = jnp.where(span < span_size - 1, total_x, width_x + rim)
     for c in range(comps):
+        pads(c, 0)
+        pads(c, 1)
         for sweep in range(1, SWEEPS + 1):
 
             def row_step(x, before, c=c):
@@ -300,7 +348,9 @@
 
             lax.fori_loop(sweep, total_x - sweep, row_step, smooth[c, sweep - 1], unroll=2)
         out[c] = smooth[c, pl.ds(rim, width_x), :, own]
-    sent(1)
+    for c in range(comps):
+        sent(c, 0)
+        sent(c, 1)
 
 
 VMEM = pl.BlockSpec(memory_space=pltpu.VMEM)
@@ -316,6 +366,13 @@
     cols = min(256, cap)
     lines = span_size * cap // cols
     block = math.gcd(part_rows, 512)
+    rim = SWEEPS
+    up = [(i, i + 1) for i in range(span_size - 1)]
+    down = [(j, i) for i, j in up]
+    edge = jnp.concatenate([prior_solid[None, :, -rim:], prior_drag[:, :, -rim:]], axis=0)
+    above = lax.ppermute(edge, "span", up)
+    edge = jnp.concatenate([prior_solid[None, :, :rim], prior_drag[:, :, :rim]], axis=0)
+    below = lax.ppermute(edge, "span", down)
     packed, slots = pl.pallas_call(
         functools.partial(pack_kernel, span_size, cap, block),
         out_shape=(
@@ -328,9 +385,7 @@
         name="pack",
     )(part_count, part_slab.reshape(1, part_rows), part_cell, part_volume, part_drag)
     per = lines // span_size
-    recv = lax.all_to_all(
-        packed.reshape(5, span_size, per, cols), "span", split_axis=1, concat_axis=1, tiled=True
-    ).reshape(5, lines, cols)
+    recv = exchange(packed.reshape(5, span_size, per, cols), 1).reshape(5, lines, cols)
     grid_rows = layers * width_x
     target = pl.pallas_call(
         functools.partial(deposit_kernel, 8, layers),
@@ -341,26 +396,25 @@
         name="deposit",
     )(recv)
     target = target.reshape(4, width_x, layers, width_y)
-    rim = SWEEPS
     wide = (4, width_x + 2 * rim, layers, width_y + 256)
     smooth = pl.pallas_call(
         functools.partial(sweeps_kernel, rim),
         out_shape=jax.ShapeDtypeStruct(target.shape, F32),
-        in_specs=[VMEM] * 3,
+        in_specs=[VMEM] * 5,
         out_specs=VMEM,
         scratch_shapes=[
             pltpu.VMEM(wide, F32),
             pltpu.VMEM(wide, F32),
             pltpu.VMEM((2, 2, 4, 8, 128), F32),
             pltpu.VMEM((2, 2, 3, 4, 8, 128), F32),
-            pltpu.SemaphoreType.DMA((2, 8)),
-            pltpu.SemaphoreType.DMA((2, 8)),
+            pltpu.SemaphoreType.DMA((4, 2, 8)),
+            pltpu.SemaphoreType.DMA((4, 2, 8)),
         ],
         compiler_params=pltpu.CompilerParams(
             vmem_limit_bytes=48 * 1024 * 1024, collective_id=0, has_side_effects=True
         ),
         name="sweeps",
-    )(prior_solid, prior_drag, target)
+    )(prior_solid, prior_drag, above, below, target)
     fields, values = pl.pallas_call(
         functools.partial(gather_kernel, 8),
         out_shape=(
@@ -373,9 +427,7 @@
         compiler_params=LIMIT,
         name="gather",
     )(smooth, recv)
-    returned = lax.all_to_all(
-        values.reshape(4, span_size, per, cols), "span", split_axis=1, concat_axis=1, tiled=True
-    ).reshape(4, lines, cols)
+    returned = exchange(values.reshape(4, span_size, per, cols), 2).reshape(4, lines, cols)
     feedback = pl.pallas_call(
         functools.partial(unpack_kernel, block),
         out_shape=jax.ShapeDtypeStruct((4, 1, part_rows), F32),

time: 155 us -> 137 us (0.88)
  blocking collectives: 35.5 us -> 0 us
  Pallas kernels: 114 us -> 127 us
  starting transfers between devices: 0 us -> 5.29 us
    all_to_all x2 -> x0, blocking collectives: 35.5 us -> none  [the longest x1 20.3 us: on_device(): lax.all_to_all(values.reshape(4, span_size, per, cols), 'span', split_axi...]
    pallas_call x0 -> x2, Pallas kernels: none -> 30.6 us  [exchange(): pl.pallas_call(functools.partial(exchange_kernel, count), out_shape=jax.S...]
    pallas_call x1, Pallas kernels: 54.9 us -> 38.2 us  [on_device(): pl.pallas_call(functools.partial(sweeps_kernel, rim), out_shape=jax.Shape...]
    ppermute x0 -> x2, starting transfers between devices: none -> 5.29 us  [the longest x1 3.99 us: on_device(): above = lax.ppermute(edge, 'span', up)]
    unnamed x12, local copies, waits for them, and re-layouts: 3.17 us -> 0.04 us
  transfers between devices with their start and end apart: 0 -> 2, of which waited for: 0 -> 0; matrix products, arithmetic and copies ran while one was open for 0% -> 0% of each run, Pallas kernels for 0% -> 32%
where the time goes in v3:
time: 137 us; the launch traced here: 136 us
  Pallas kernels  127 us (93%)
  starting transfers between devices  5.29 us (4%)
  local copies, waits for them, and re-layouts  2.23 us (2%)
  between operations  1.47 us (1%)
    pallas_call x1, Pallas kernels, on_device(): pl.pallas_call(functools.partial(sweeps_kernel, rim), out_shape=jax.Shape...  38.2 us
    pallas_call x2, Pallas kernels, exchange(): pl.pallas_call(functools.partial(exchange_kernel, count), out_shape=jax.S...  30.6 us
    pallas_call x1, Pallas kernels, on_device(): pl.pallas_call(functools.partial(gather_kernel, 8), out_shape=(jax.ShapeD...  22.4 us
    pallas_call x1, Pallas kernels, on_device(): pl.pallas_call(functools.partial(deposit_kernel, 8, layers), out_shape=ja...  20.3 us
    pallas_call x1, Pallas kernels, on_device(): pl.pallas_call(functools.partial(pack_kernel, span_size, cap, block), out...  9.79 us
    pallas_call x1, Pallas kernels, on_device(): pl.pallas_call(functools.partial(unpack_kernel, block), out_shape=jax.Sha...  6.09 us
    ppermute x1, starting transfers between devices, on_device(): above = lax.ppermute(edge, 'span', up)  3.99 us
  transfers between devices with their start and end apart: 2, of which 0 were waited for; matrix products, arithmetic and copies ran while one was open for 0% of the time, Pallas kernels for 32%

profile of v3, /device:TPU:1, one launch (start us, length us, event | category | flops | bytes accessed | tf_op | source)
XLA Modules:
  0.0 136.4 jit_solution(6148727810777758917)
XLA Ops:
  0.6 1.0 slice_bitcast_fusion
  1.6 1.2 fusion
  2.8 0.1 pad_maximum_fusion
  2.9 4.0 %collective-permute-start = (f32[4,8,6,512]{3,2,1,0:T(8,128)S(1)}, f32[4,8,6,512]{3,2,1,0:T(8,128)S(1)}, u32[]{:S(2)}, u32[]{:S(2)}) collective-permute-start(f32[4,8,6,512]{3,2,1,0:T(8,128)S(1)} %pad_maximum_fusion), channel_id=1, source_target_pairs={{0,4},{4,8},{8,12},{12,16},{16,20},{20,24},{24,28},{1,5},{5,9},{9,... | collective-permute-start | bytes 1179656 | tf_op jit(solution)/shard_map/ppermute | solution.py:373
  6.9 0.0 copy-start.2
  6.9 0.0 copy-start.3
  6.9 0.0 copy-start.4
  6.9 0.0 copy-start.5
  6.9 0.1 pad_maximum_fusion.1
  7.0 1.3 collective-permute-start.1
  9.0 0.0 copy-done.2
  9.0 0.0 copy-done.3
  9.0 0.0 copy-done.4
  9.0 0.0 copy-done.5
  9.0 9.8 %pack.1 = (f32[5,64,256]{2,1,0:T(8,128)S(1)}, s32[1,8192]{1,0:T(1,128)S(1)}) custom-call(s32[1,1]{1,0:T(1,128)S(6)} %copy.9.count, s32[1,8192]{1,0:T(1,128)S(1)} %bitcast.16, s32[1,8192]{1,0:T(1,128)S(1)} %copy-done.4, f32[1,8192]{1,0:T(1,128)S(1)} %copy-done.5, f32[3,1,8192]{2,1,0:T(1,128)S(1)} %copy-done.2), custom_call_target="tpu_custom_call" | custom-call | tf_op jit(solution)/shard_map/pack/pallas_call | solution.py:376
  18.8 13.6 %exchange_1.1 = f32[5,8,8,256]{3,2,1,0:T(8,128)S(1)} custom-call(f32[5,8,8,256]{3,2,1,0:T(8,128)S(1)} %bitcast.14), custom_call_target="tpu_custom_call" | custom-call | tf_op jit(solution)/shard_map/exchange_1/pallas_call | solution.py:191
  32.4 0.0 copy-start
  32.4 0.0 copy-start.1
  32.4 20.3 %deposit.1 = f32[4,128,512]{2,1,0:T(8,128)S(1)} custom-call(f32[5,64,256]{2,1,0:T(8,128)S(1)} %bitcast.11), custom_call_target="tpu_custom_call" | custom-call | tf_op jit(solution)/shard_map/deposit/pallas_call | solution.py:390
  52.7 0.0 collective-permute-done.above
  52.7 0.0 collective-permute-done.1.below
  52.7 0.0 copy-done
  52.7 0.0 copy-done.1
  52.7 38.2 %sweeps.1.smooth = f32[4,16,8,512]{3,2,1,0:T(8,128)S(1)} custom-call(f32[8,16,512]{2,1,0:T(8,128)S(1)} %copy-done.1, f32[3,8,16,512]{3,2,1,0:T(8,128)S(1)} %copy-done, f32[4,8,6,512]{3,2,1,0:T(8,128)S(1)} %collective-permute-done.above, f32[4,8,6,512]{3,2,1,0:T(8,128)S(1)} %collective-permute-done.1.below, f32[4,16,8,512]{3,2,1,0:T(8,128)S(1)} %bitcast.10), custom_call_target="tpu_custom_call" | custom-call | tf_op jit(solution)/shard_map/sweeps/pallas_call | solution.py:400
  90.9 22.4 %gather.1 = (f32[4,8,16,512]{3,2,1,0:T(8,128)}, f32[4,64,256]{2,1,0:T(8,128)S(1)}) custom-call(f32[4,16,8,512]{3,2,1,0:T(8,128)S(1)} %sweeps.1.smooth, f32[5,64,256]{2,1,0:T(8,128)S(1)} %bitcast.12), custom_call_target="tpu_custom_call" | custom-call | tf_op jit(solution)/shard_map/gather/pallas_call | solution.py:418
  113.3 17.0 %exchange_2.1 = f32[4,8,8,256]{3,2,1,0:T(8,128)S(1)} custom-call(f32[4,8,8,256]{3,2,1,0:T(8,128)S(1)} %bitcast.15), custom_call_target="tpu_custom_call" | custom-call | tf_op jit(solution)/shard_map/exchange_2/pallas_call | solution.py:191
  130.3 6.1 %unpack.1 = f32[4,1,8192]{2,1,0:T(1,128)} custom-call(f32[4,64,256]{2,1,0:T(8,128)S(1)} %bitcast.13, s32[1,8192]{1,0:T(1,128)S(1)} %get-tuple-element.9.slots), custom_call_target="tpu_custom_call" | custom-call | tf_op jit(solution)/shard_map/unpack/pallas_call | solution.py:431
Async XLA Ops:
  2.9 49.8 %collective-permute-start = (f32[4,8,6,512]{3,2,1,0:T(8,128)S(1)}, f32[4,8,6,512]{3,2,1,0:T(8,128)S(1)}, u32[]{:S(2)}, u32[]{:S(2)}) collective-permute-start(f32[4,8,6,512]{3,2,1,0:T(8,128)S(1)} %pad_maximum_fusion), channel_id=1, source_target_pairs={{0,4},{4,8},{8,12},{12,16},{16,20},{20,24},{24,28},{1,5},{5,9},{9,... | collective-permute-start | bytes 1179656 | tf_op jit(solution)/shard_map/ppermute | solution.py:373
  6.9 2.1 %copy-start.2 = (f32[3,1,8192]{2,1,0:T(1,128)S(1)}, f32[3,1,8192]{2,1,0:T(1,128)}, u32[]{:S(2)}) copy-start(f32[3,1,8192]{2,1,0:T(1,128)} %drag.2) | copy-start | bytes 294916
  6.9 2.1 %copy-start.3 = (s32[1,8192,1]{1,2,0:T(1,128)S(1)}, s32[1,8192,1]{1,2,0:T(1,128)}, u32[]{:S(2)}) copy-start(s32[1,8192,1]{1,2,0:T(1,128)} %param.7) | copy-start | bytes 98308
  6.9 2.1 %copy-start.4 = (s32[1,8192]{1,0:T(1,128)S(1)}, s32[1,8192]{1,0:T(1,128)}, u32[]{:S(2)}) copy-start(s32[1,8192]{1,0:T(1,128)} %cell.1) | copy-start | bytes 98308
  6.9 2.1 %copy-start.5 = (f32[1,8192]{1,0:T(1,128)S(1)}, f32[1,8192]{1,0:T(1,128)}, u32[]{:S(2)}) copy-start(f32[1,8192]{1,0:T(1,128)} %volume.1) | copy-start | bytes 98308
  7.0 45.7 %collective-permute-start.1 = (f32[4,8,6,512]{3,2,1,0:T(8,128)S(1)}, f32[4,8,6,512]{3,2,1,0:T(8,128)S(1)}, u32[]{:S(2)}, u32[]{:S(2)}) collective-permute-start(f32[4,8,6,512]{3,2,1,0:T(8,128)S(1)} %pad_maximum_fusion.1), channel_id=1, source_target_pairs={{4,0},{8,4},{12,8},{16,12},{20,16},{24,20},{28,24},{5,1},{9,5},{13... | collective-permute-start | bytes 1179656 | tf_op jit(solution)/shard_map/ppermute | solution.py:375
  32.4 20.3 %copy-start = (f32[3,8,16,512]{3,2,1,0:T(8,128)S(1)}, f32[3,8,16,512]{3,2,1,0:T(8,128)}, u32[]{:S(2)}) copy-start(f32[3,8,16,512]{3,2,1,0:T(8,128)} %drag.3) | copy-start | bytes 2359300
  32.4 20.3 %copy-start.1 = (f32[8,16,512]{2,1,0:T(8,128)S(1)}, f32[8,16,512]{2,1,0:T(8,128)}, u32[]{:S(2)}) copy-start(f32[8,16,512]{2,1,0:T(8,128)} %solid.1) | copy-start | bytes 786436
